TPU v7x, 128 devices: a whole 4x4x4 slice. The times are simulated.
128 devices in a mesh: row: 8 (over x, core), col: 16 (over y, z).
Axes of the slice: x: 4, y: 4, z: 4, core: 2. Of those that a mesh axis runs over, the one named last changes fastest.
Arguments:
- vectors: float32 [131072, 768], P(('row', 'col')), may hold values from -6 to 6
- list_ids: int32 [131072], P(('row', 'col')), may hold values from 0 to 65535, as said below
- pq_codes: int32 [131072, 96], P(('row', 'col')), may hold values from 0 to 255
- fill_counts: int32 [128, 128], P(('row', 'col')), may hold values from 0 to 8, as said below
- centroids: float32 [65536, 768], P(('row', 'col')), may hold values from -6 to 6
- codebook: float32 [96, 8, 256], P('col'), may hold values from -6 to 6
Outputs:
- coded_err: float32 [131072], P(('row', 'col'))
- best_err: float32 [131072], P(('row', 'col'))
Inputs may be any that keep to these rules, and one draw needn't show every extreme that they name: `list_ids`: slot s of device p lies in block s // 8, which belongs to owner device s // 8 (devices numbered row-major over row and col); it names a list of that owner, from (s // 8) * 512 to (s // 8 + 1) * 512 - 1. fill_counts[p, d] is the number of live slots at the head of device p's block for owner d; some owner receives 8 live slots from every device.
All inputs are finite; a program needn't handle non-finite values.
Results may differ from a plain program's by a relative error of at most 0.0003.
Values sent between devices are 32-bit elements; how exact they have to be, the bound alone decides.
No kernel may reach another device: no remote copies, remote signals or barrier semaphores. Data moves between devices by JAX's collectives and lax.ppermute only.
A program may use at most 256 MiB of HBM per device.

v0:
```python
import math

import jax
import jax.numpy as jnp
from jax import lax
from jax.sharding import PartitionSpec as P


def sent_together(arrays, axis, split_dim, concat_dim, along):
    widths = [math.prod(a.shape[along:]) for a in arrays]
    both = jnp.concatenate(
        [a.reshape(*a.shape[:along], w) for a, w in zip(arrays, widths)], axis=along
    )
    out = lax.all_to_all(both, axis, split_axis=split_dim, concat_axis=concat_dim, tiled=True)
    parts = jnp.split(out, [sum(widths[:k]) for k in range(1, len(widths))], axis=along)
    return tuple((b.reshape(*out.shape[:along], *a.shape[along:]) for a, b in zip(arrays, parts)))


def laid_out(parts, dim):
    shape = list(parts.shape[1:])
    shape[dim] *= parts.shape[0]
    return jnp.moveaxis(parts, 0, dim).reshape(shape)


def copy_for_each(value, axis):
    count = lax.axis_size(axis)
    return lax.all_to_all(
        jnp.broadcast_to(value[None], (count, *value.shape)), axis, 0, 0, tiled=True
    )


def gather_directly(value, axis, dim):
    return laid_out(copy_for_each(value, axis), dim)


def sent_together_2(arrays, axis, split_dim, concat_dim, along):
    ends, at = ([], 0)
    for a in arrays[:-1]:
        at += a.shape[along]
        ends.append(at)
    both = jnp.concatenate(arrays, axis=along)
    return tuple(
        jnp.split(
            lax.all_to_all(both, axis, split_axis=split_dim, concat_axis=concat_dim, tiled=True),
            ends,
            axis=along,
        )
    )


def block_terms(block_vec, block_codes, shard_piece, code_norms):
    resid_norms = jnp.sum(block_vec * block_vec, axis=2)
    cross_term = jnp.einsum("bms,msk->bmk", block_vec, shard_piece, precision=lax.Precision.HIGHEST)
    dist_table = resid_norms[:, :, None] - 2.0 * cross_term + code_norms[None, :, :]
    best_sum = jnp.sum(jnp.min(dist_table, axis=2), axis=1)
    code_index = lax.broadcasted_iota(jnp.int32, dist_table.shape, 2)
    coded_sum = jnp.sum(
        jnp.where(code_index == block_codes[:, :, None], dist_table, 0.0), axis=(1, 2)
    )
    return jnp.stack([coded_sum, best_sum])


def local(vectors, list_ids, pq_codes, fill_counts, centroids, codebook):
    row_count = lax.axis_size("row")
    col_count = lax.axis_size("col")
    device_count = row_count * col_count
    slot_count = vectors.shape[0]
    capacity = slot_count // device_count
    feature_width = vectors.shape[1]
    sub_total = pq_codes.shape[1]
    sub_width = feature_width // sub_total
    out_vec = vectors.reshape(device_count, capacity, feature_width)
    out_ids = list_ids.reshape(device_count, capacity)
    out_codes = pq_codes.reshape(device_count, capacity, sub_total)
    got_vec, got_ids, got_codes = (
        lax.all_to_all(out_vec, ("row", "col"), split_axis=0, concat_axis=0, tiled=True),
        *sent_together((out_ids, out_codes), ("row", "col"), 0, 0, 2),
    )
    got_vec = got_vec.reshape(slot_count, feature_width)
    got_ids = got_ids.reshape(slot_count)
    got_codes = got_codes.reshape(slot_count, sub_total)
    residual = got_vec - jnp.take(centroids, got_ids % centroids.shape[0], axis=0)
    block_rows = 128
    block_count = slot_count // block_rows
    shard_piece = gather_directly(codebook, "col", 0)
    sub_count = shard_piece.shape[0]
    code_norms = jnp.sum(shard_piece * shard_piece, axis=1)
    shaped = residual.reshape(block_count, block_rows, sub_count, sub_width)
    shaped_codes = got_codes.reshape(block_count, block_rows, sub_count)

    def one_block(pair):
        return block_terms(pair[0], pair[1], shard_piece, code_norms)

    parts = lax.map(one_block, (shaped, shaped_codes))
    totals = jnp.transpose(parts, (1, 0, 2)).reshape(2, slot_count)
    coded_sum = totals[0]
    best_sum = totals[1]
    back_coded, back_best = sent_together_2(
        (coded_sum.reshape(device_count, capacity), best_sum.reshape(device_count, capacity)),
        ("row", "col"),
        0,
        0,
        1,
    )
    slot_pos = jnp.arange(capacity, dtype=jnp.int32)
    live_mask = slot_pos[None, :] < fill_counts[0][:, None]
    coded_err = jnp.where(live_mask, back_coded, 0.0).reshape(slot_count)
    best_err = jnp.where(live_mask, back_best, 0.0).reshape(slot_count)
    return (coded_err, best_err)


def solution(mesh):
    in_specs = (
        P(("row", "col"), None),
        P(("row", "col")),
        P(("row", "col"), None),
        P(("row", "col"), None),
        P(("row", "col"), None),
        P("col", None, None),
    )
    out_specs = (P(("row", "col")), P(("row", "col")))
    return jax.shard_map(local, mesh=mesh, in_specs=in_specs, out_specs=out_specs, check_vma=False)
```

profile of v0, /device:TPU:1, one launch (start us, length us, event | category | flops | bytes accessed | tf_op | source)
XLA Modules:
  0.0 403.3 jit_solution(954442653757924704)
XLA Ops:
  0.6 1.3 copy.24
  3.2 25.1 %all_to_all.27 = s32[128,8,97]{2,1,0:T(8,128)S(1)} all-to-all(s32[128,8,97]{2,1,0:T(8,128)S(1)} %pad_add_fusion), channel_id=1, replica_groups=mesh['row'=8,'col'=16] {'row','col'}, dimensions={0} | all-to-all | bytes 794624 | tf_op jit(solution)/shard_map/all_to_all | solution.py:14
  29.2 16.0 %all_to_all.28 = f32[16,6,8,256]{3,2,1,0:T(8,128)S(1)} all-to-all(f32[16,6,8,256]{3,2,1,0:T(8,128)S(1)} %broadcast_in_dim.39), channel_id=1, replica_groups=mesh['row'=8,'col'=16] {'col'}, dimensions={0} | all-to-all | bytes 1572864 | tf_op jit(solution)/shard_map/all_to_all | solution.py:27
  45.2 6.2 %all-to-all-start.1 = ((f32[128,8,768]{2,1,0:T(8,128)}), f32[128,8,768]{2,1,0:T(8,128)}, u32[]{:S(2)}, u32[]{:S(2)}) async-start(f32[128,8,768]{2,1,0:T(8,128)} %bitcast.52), calls=%async_computation.1 | async-start | bytes 6291456 | tf_op jit(solution)/shard_map/all_to_all | solution.py:76
  51.4 2.2 slice_reduce_fusion
  55.1 5.3 %gather_fusion = f32[1024,768]{1,0:T(8,128)} fusion(f32[512,768]{1,0:T(8,128)S(1)} %copy-done, s32[1024]{0:T(1024)S(1)} %broadcast_clamp_fusion), kind=kCustom, calls=%fused_computation | custom fusion | bytes 6295552 | tf_op jit(solution)/shard_map/jit(_take)/gather | solution.py:82
  60.3 31.0 %reshape.125 = f32[8,128,96,8]{3,2,1,0:T(8,128)} reshape(f32[1024,768]{1,0:T(8,128)} %gather_fusion) | data formatting | bytes 6291456 | tf_op jit(solution)/shard_map/jit(_take)/gather | solution.py:82
  92.0 31.1 %reshape.113 = f32[8,128,96,8]{3,2,1,0:T(8,128)} reshape(f32[128,8,768]{2,1,0:T(8,128)} %all-to-all-done.1) | data formatting | bytes 6291456 | tf_op jit(solution)/shard_map/reshape | solution.py:79
  123.0 49.1 %select_subtract_fusion = f32[8,128,96,8]{3,2,1,0:T(8,128)} fusion(f32[8,128,96,8]{3,2,1,0:T(8,128)} %reshape.113, f32[8,128,96,8]{3,2,1,0:T(8,128)} %reshape.125, pred[8,128]{1,0:T(8,128)(4,1)S(1)} %compare_and_fusion), kind=kLoop, calls=%fused_computation.15 | loop fusion | flops 1572864 | bytes 9438208 | tf_op jit(solution)/shard_map/sub | solution.py:82
  172.1 35.4 %copy.29 = f32[8,128,96,8]{1,3,2,0:T(8,128)} copy(f32[8,128,96,8]{3,2,1,0:T(8,128)} %select_subtract_fusion) | data formatting | bytes 6291456 | tf_op jit(solution)/shard_map/while | solution.py:94
  207.5 175.0 %while.10 = (s32[]{:T(128)}, f32[8,2,128]{2,1,0:T(2,128)S(1)}, s32[8,128,96]{1,2,0:T(8,128)}, f32[8,128,96,8]{1,3,2,0:T(8,128)}, f32[96,8,256]{2,1,0:T(8,128)S(1...) while((s32[]{:T(128)}, f32[8,2,128]{2,1,0:T(2,128)S(1)}, s32[8,128,96]{1,2,0:T(8,128)}, ...), condition=%wide.region_6.7_spmd, body=%wide.region_1.0_spmd.sunk | while | flops 324194304 | bytes 2018417 | solution.py:94
  207.5 1.1 fusion.15
  209.5 19.9 %select_reduce_fusion.2 = (f32[128]{0:T(128)S(1)}, f32[128,96]{0,1:T(8,128)S(1)}) fusion(f32[96,256]{1,0:T(8,128)S(1)} %get-tuple-element.133, f32[128,96]{0,1:T(8,128)S(1)} %fusion.15, s32[128,96]{0,1:T(8,128)S(1)} %dynamic-slice_bitcast_fusion.2, f32[96,8,256]{2,1,0:T(8,128)S(1)} %get-tuple-element.132, f32[8,128,96,8]{1,3,2,0:T(8,128)} %get-tuple-element.131, ...), kind=kOutput, calls=%fused_computation.3.clone.1 | convolution fusion | flops 323997568 | bytes 1425924 | tf_op jit(solution)/shard_map/while/body/eval_jaxpr/bms,msk->bmk/dot_general | solution.py:53
  229.4 1.1 fusion.15
  231.3 19.9 %select_reduce_fusion.2 = (f32[128]{0:T(128)S(1)}, f32[128,96]{0,1:T(8,128)S(1)}) fusion(f32[96,256]{1,0:T(8,128)S(1)} %get-tuple-element.133, f32[128,96]{0,1:T(8,128)S(1)} %fusion.15, s32[128,96]{0,1:T(8,128)S(1)} %dynamic-slice_bitcast_fusion.2, f32[96,8,256]{2,1,0:T(8,128)S(1)} %get-tuple-element.132, f32[8,128,96,8]{1,3,2,0:T(8,128)} %get-tuple-element.131, ...), kind=kOutput, calls=%fused_computation.3.clone.1 | convolution fusion | flops 323997568 | bytes 1425924 | tf_op jit(solution)/shard_map/while/body/eval_jaxpr/bms,msk->bmk/dot_general | solution.py:53
  253.2 19.9 %select_reduce_fusion.2 = (f32[128]{0:T(128)S(1)}, f32[128,96]{0,1:T(8,128)S(1)}) fusion(f32[96,256]{1,0:T(8,128)S(1)} %get-tuple-element.133, f32[128,96]{0,1:T(8,128)S(1)} %fusion.15, s32[128,96]{0,1:T(8,128)S(1)} %dynamic-slice_bitcast_fusion.2, f32[96,8,256]{2,1,0:T(8,128)S(1)} %get-tuple-element.132, f32[8,128,96,8]{1,3,2,0:T(8,128)} %get-tuple-element.131, ...), kind=kOutput, calls=%fused_computation.3.clone.1 | convolution fusion | flops 323997568 | bytes 1425924 | tf_op jit(solution)/shard_map/while/body/eval_jaxpr/bms,msk->bmk/dot_general | solution.py:53
  273.2 1.1 fusion.15
  275.1 19.9 %select_reduce_fusion.2 = (f32[128]{0:T(128)S(1)}, f32[128,96]{0,1:T(8,128)S(1)}) fusion(f32[96,256]{1,0:T(8,128)S(1)} %get-tuple-element.133, f32[128,96]{0,1:T(8,128)S(1)} %fusion.15, s32[128,96]{0,1:T(8,128)S(1)} %dynamic-slice_bitcast_fusion.2, f32[96,8,256]{2,1,0:T(8,128)S(1)} %get-tuple-element.132, f32[8,128,96,8]{1,3,2,0:T(8,128)} %get-tuple-element.131, ...), kind=kOutput, calls=%fused_computation.3.clone.1 | convolution fusion | flops 323997568 | bytes 1425924 | tf_op jit(solution)/shard_map/while/body/eval_jaxpr/bms,msk->bmk/dot_general | solution.py:53
  297.0 19.9 %select_reduce_fusion.2 = (f32[128]{0:T(128)S(1)}, f32[128,96]{0,1:T(8,128)S(1)}) fusion(f32[96,256]{1,0:T(8,128)S(1)} %get-tuple-element.133, f32[128,96]{0,1:T(8,128)S(1)} %fusion.15, s32[128,96]{0,1:T(8,128)S(1)} %dynamic-slice_bitcast_fusion.2, f32[96,8,256]{2,1,0:T(8,128)S(1)} %get-tuple-element.132, f32[8,128,96,8]{1,3,2,0:T(8,128)} %get-tuple-element.131, ...), kind=kOutput, calls=%fused_computation.3.clone.1 | convolution fusion | flops 323997568 | bytes 1425924 | tf_op jit(solution)/shard_map/while/body/eval_jaxpr/bms,msk->bmk/dot_general | solution.py:53
  318.9 19.9 %select_reduce_fusion.2 = (f32[128]{0:T(128)S(1)}, f32[128,96]{0,1:T(8,128)S(1)}) fusion(f32[96,256]{1,0:T(8,128)S(1)} %get-tuple-element.133, f32[128,96]{0,1:T(8,128)S(1)} %fusion.15, s32[128,96]{0,1:T(8,128)S(1)} %dynamic-slice_bitcast_fusion.2, f32[96,8,256]{2,1,0:T(8,128)S(1)} %get-tuple-element.132, f32[8,128,96,8]{1,3,2,0:T(8,128)} %get-tuple-element.131, ...), kind=kOutput, calls=%fused_computation.3.clone.1 | convolution fusion | flops 323997568 | bytes 1425924 | tf_op jit(solution)/shard_map/while/body/eval_jaxpr/bms,msk->bmk/dot_general | solution.py:53
  338.8 1.1 fusion.15
  340.7 19.9 %select_reduce_fusion.2 = (f32[128]{0:T(128)S(1)}, f32[128,96]{0,1:T(8,128)S(1)}) fusion(f32[96,256]{1,0:T(8,128)S(1)} %get-tuple-element.133, f32[128,96]{0,1:T(8,128)S(1)} %fusion.15, s32[128,96]{0,1:T(8,128)S(1)} %dynamic-slice_bitcast_fusion.2, f32[96,8,256]{2,1,0:T(8,128)S(1)} %get-tuple-element.132, f32[8,128,96,8]{1,3,2,0:T(8,128)} %get-tuple-element.131, ...), kind=kOutput, calls=%fused_computation.3.clone.1 | convolution fusion | flops 323997568 | bytes 1425924 | tf_op jit(solution)/shard_map/while/body/eval_jaxpr/bms,msk->bmk/dot_general | solution.py:53
  362.6 19.9 %select_reduce_fusion.2 = (f32[128]{0:T(128)S(1)}, f32[128,96]{0,1:T(8,128)S(1)}) fusion(f32[96,256]{1,0:T(8,128)S(1)} %get-tuple-element.133, f32[128,96]{0,1:T(8,128)S(1)} %fusion.15, s32[128,96]{0,1:T(8,128)S(1)} %dynamic-slice_bitcast_fusion.2, f32[96,8,256]{2,1,0:T(8,128)S(1)} %get-tuple-element.132, f32[8,128,96,8]{1,3,2,0:T(8,128)} %get-tuple-element.131, ...), kind=kOutput, calls=%fused_computation.3.clone.1 | convolution fusion | flops 323997568 | bytes 1425924 | tf_op jit(solution)/shard_map/while/body/eval_jaxpr/bms,msk->bmk/dot_general | solution.py:53
  382.9 19.0 %all_to_all.29 = f32[128,1,16]{2,1,0:T(1,128)S(1)} all-to-all(f32[128,1,16]{2,1,0:T(1,128)S(1)} %bitcast.57), channel_id=1, replica_groups=mesh['row'=8,'col'=16] {'row','col'}, dimensions={0} | all-to-all | bytes 16384 | tf_op jit(solution)/shard_map/all_to_all | solution.py:44
  (55 shorter events, 17.1 us)
Async XLA Ops:
  0.6 54.4 %copy-start = (f32[512,768]{1,0:T(8,128)S(1)}, f32[512,768]{1,0:T(8,128)}, u32[]{:S(2)}) copy-start(f32[512,768]{1,0:T(8,128)} %param.12) | copy-start | bytes 4718596
  45.2 46.8 %all-to-all-start.1 = ((f32[128,8,768]{2,1,0:T(8,128)}), f32[128,8,768]{2,1,0:T(8,128)}, u32[]{:S(2)}, u32[]{:S(2)}) async-start(f32[128,8,768]{2,1,0:T(8,128)} %bitcast.52), calls=%async_computation.1 | async-start | bytes 6291456 | tf_op jit(solution)/shard_map/all_to_all | solution.py:76
  207.5 194.3 %copy-start.2 = (s32[1,128]{1,0:T(1,128)S(1)}, s32[1,128]{1,0:T(1,128)}, u32[]{:S(2)}) copy-start(s32[1,128]{1,0:T(1,128)} %param.11) | copy-start | bytes 1540
  382.6 20.8 %copy-start.1 = (f32[512,768]{1,0:T(8,128)S(1)}, f32[512,768]{1,0:T(8,128)}, u32[]{:S(2)}) copy-start(f32[512,768]{1,0:T(8,128)} %param.12) | copy-start | bytes 4718596
where the time goes:
time: 406 us; the launch traced here: 403 us
  matrix products  159 us (39%)
  local copies, waits for them, and re-layouts  118 us (29%)
  blocking collectives  60.1 us (15%)
  other arithmetic  59 us (15%)
  starting transfers between devices  6.22 us (2%)
    dot_general x8, matrix products, block_terms(): jnp.einsum('bms,msk->bmk', block_vec, shard_piece, precision=lax.Precisio...  159 us
    sub x1, other arithmetic, local(): got_vec - jnp.take(centroids, got_ids % centroids.shape[0], axis=0)  49.1 us
    while x2, local copies, waits for them, and re-layouts, local(): parts = lax.map(one_block, (shaped, shaped_codes))  36.3 us
    gather x2, local copies, waits for them, and re-layouts, local(): jnp.take(centroids, got_ids % centroids.shape[0], axis=0)  36.3 us
    reshape x1, local copies, waits for them, and re-layouts, local(): got_vec = got_vec.reshape(slot_count, feature_width)  31.1 us
    all_to_all x1, blocking collectives, sent_together(): lax.all_to_all(both, axis, split_axis=split_dim, concat_axis=concat_dim,...  25.1 us
    all_to_all x1, blocking collectives, sent_together_2(): lax.all_to_all(both, axis, split_axis=split_dim, concat_axis=concat_dim,...  19 us
    all_to_all x1, blocking collectives, copy_for_each(): lax.all_to_all(jnp.broadcast_to(value[None], (count, *value.shape)), axis...  16 us
  transfers between devices with their start and end apart: 1, of which 1 were waited for; matrix products, arithmetic and copies ran while one was open for 10% of the time, Pallas kernels for 0%

commit v1 on v0

v1 whole, which is shorter than its diff:
```python
import functools

import jax
import jax.numpy as jnp
from jax import lax
from jax.experimental import pallas as pl
from jax.experimental.pallas import tpu as pltpu
from jax.sharding import PartitionSpec as P

BOTH = ("row", "col")
LANES = 128
SPLITS = 64


def three_way(x):
    hi = x.astype(jnp.bfloat16).astype(jnp.float32)
    rest = x - hi
    mid = rest.astype(jnp.bfloat16).astype(jnp.float32)
    lo = (rest - mid).astype(jnp.bfloat16).astype(jnp.float32)
    return hi, mid, lo


def prep_kernel(core_ref, vec_ref, codes_ref, own_ref, sib_ref, vt_ref, wt_ref, a_ref):
    step = pl.program_id(0)
    core = core_ref[0]
    rows = vec_ref.shape[0]
    sublane = lax.broadcasted_iota(jnp.int32, (8, 256), 0)
    lane = lax.broadcasted_iota(jnp.int32, (256, LANES), 1)
    for g in range(rows // LANES):
        vt_ref[:, g * LANES : (g + 1) * LANES] = vec_ref[g * LANES : (g + 1) * LANES, :].T
    stacks = []
    for i in range(16):
        m = step * 16 + i
        shard, within = m // 6, m % 6
        half, j = within // 3, within % 3
        base = shard * 8 + j * 2
        mine = half == core
        words = []
        for h in range(2):
            spot = pl.ds(base + h, 8, stride=LANES)
            words.append(jnp.where(mine, own_ref[spot, :], sib_ref[spot, :]))
        for g in range(rows // LANES):
            cut = slice(g * LANES, (g + 1) * LANES)
            code = jnp.broadcast_to(codes_ref[i : i + 1, cut], (8, LANES))
            low = code & (LANES - 1)
            first = jnp.take_along_axis(words[0], low, axis=1, mode="promise_in_bounds")
            second = jnp.take_along_axis(words[1], low, axis=1, mode="promise_in_bounds")
            word = jnp.where(code >= LANES, second, first)
            wt_ref[i * 8 : (i + 1) * 8, cut] = vt_ref[i * 8 : (i + 1) * 8, cut] - word
        both = jnp.concatenate(words, axis=1)
        norm = jnp.sum(both * both, axis=0, keepdims=True)
        hi, mid, lo = three_way(-2.0 * both)
        nhi, nmid, nlo = three_way(norm)
        norms = jnp.where(sublane == 0, nhi, jnp.where(sublane == 1, nmid, jnp.where(sublane == 2, nlo, 0.0)))
        stacks.append([hi, hi, hi, mid, mid, lo, norms, jnp.zeros_like(norms)])
        if i % 2 == 1:
            turned = jnp.concatenate(stacks[0] + stacks[1], axis=0).T
            a_ref[i - 1] = jnp.where(lane < SPLITS, turned, 0.0).astype(jnp.bfloat16)
            a_ref[i] = jnp.where(lane < SPLITS, 0.0, turned).astype(jnp.bfloat16)
            stacks = []


def score_kernel(vt_ref, wt_ref, cent_ref, a_ref, live_ref, coded_ref, best_ref, acc_ref):
    step = pl.program_id(0)
    rows = cent_ref.shape[0]
    wide = 256

    @pl.when(step == 0)
    def _():
        acc_ref[...] = jnp.zeros_like(acc_ref)

    ones = jnp.ones((16, wide), jnp.bfloat16)
    for t in range(rows // wide):
        cut = slice(t * wide, (t + 1) * wide)
        turned = jnp.concatenate(
            [cent_ref[t * wide + g * LANES : t * wide + (g + 1) * LANES, :].T for g in range(wide // LANES)],
            axis=1,
        )
        resid = vt_ref[:, cut] - turned
        err = wt_ref[:, cut] - turned
        acc_ref[0:8, cut] += jnp.sum((err * err).reshape(16, 8, wide), axis=0)
        acc_ref[8:16, cut] += jnp.sum((resid * resid).reshape(16, 8, wide), axis=0)
        least = jnp.zeros((1, wide), jnp.float32)
        for pair in range(8):
            side = []
            for half in range(2):
                at = (pair * 2 + half) * 8
                hi, mid, lo = three_way(resid[at : at + 8, :])
                side += [
                    jnp.concatenate([hi, mid], axis=0).astype(jnp.bfloat16),
                    jnp.concatenate([lo, hi], axis=0).astype(jnp.bfloat16),
                    jnp.concatenate([mid, hi], axis=0).astype(jnp.bfloat16),
                    ones,
                ]
            right = jnp.concatenate(side, axis=0)
            for half in range(2):
                table = jnp.dot(a_ref[pair * 2 + half], right, preferred_element_type=jnp.float32)
                least += jnp.min(table, axis=0, keepdims=True)
        acc_ref[16:17, cut] += least

    @pl.when(step == pl.num_programs(0) - 1)
    def _():
        live = live_ref[...] != 0
        coded = jnp.sum(acc_ref[0:8, :], axis=0, keepdims=True)
        best = jnp.sum(acc_ref[8:16, :], axis=0, keepdims=True) + acc_ref[16:17, :]
        coded_ref[...] = jnp.where(live, coded, 0.0)
        best_ref[...] = jnp.where(live, best, 0.0)


def local(vectors, list_ids, pq_codes, fill_counts, centroids, codebook):
    row_count = lax.axis_size("row")
    col_count = lax.axis_size("col")
    devices = row_count * col_count
    slots, width = vectors.shape
    cap = slots // devices
    subs = pq_codes.shape[1]
    f32 = jnp.float32
    my_row = lax.axis_index("row")
    core = my_row % 2

    coord = lax.dynamic_index_in_dim(codebook, my_row, axis=1, keepdims=False)
    halves = coord.reshape(2, 6, LANES)
    piece = jnp.broadcast_to(halves[None, :, None], (row_count // 2, 2, col_count, 6, LANES))
    piece = piece.reshape(devices, 6, LANES)
    ids = (list_ids.reshape(devices, 1, cap) % centroids.shape[0]).astype(f32)
    ids = jnp.pad(ids, ((0, 0), (0, 1), (0, LANES - cap)))
    sent = jnp.concatenate([piece, ids], axis=1)
    got = lax.all_to_all(sent, BOTH, 0, 0, tiled=True)
    sibling = lax.ppermute(got, "row", [(i, i ^ 1) for i in range(row_count)])

    want = got[:, 6, :cap].astype(jnp.int32).reshape(slots)
    picked = centroids.at[want].get(mode="promise_in_bounds")
    cent = lax.all_to_all(picked.reshape(devices, cap, width), BOTH, 0, 0, tiled=True)
    cent = cent.reshape(slots, width)

    steps = width // LANES
    per = subs // steps
    vt, wt, a = pl.pallas_call(
        prep_kernel,
        grid=(steps,),
        in_specs=[
            pl.BlockSpec(memory_space=pltpu.SMEM),
            pl.BlockSpec((slots, LANES), lambda i: (0, i)),
            pl.BlockSpec((per, slots), lambda i: (i, 0)),
            pl.BlockSpec((devices * 8, LANES), lambda i: (0, 0)),
            pl.BlockSpec((devices * 8, LANES), lambda i: (0, 0)),
        ],
        out_specs=[
            pl.BlockSpec((LANES, slots), lambda i: (i, 0)),
            pl.BlockSpec((LANES, slots), lambda i: (i, 0)),
            pl.BlockSpec((per, 256, LANES), lambda i: (i, 0, 0)),
        ],
        out_shape=[
            jax.ShapeDtypeStruct((width, slots), f32),
            jax.ShapeDtypeStruct((width, slots), f32),
            jax.ShapeDtypeStruct((subs, 256, LANES), jnp.bfloat16),
        ],
        name="prep",
    )(
        core.reshape(1).astype(jnp.int32),
        vectors,
        pq_codes.T,
        got.reshape(devices * 8, LANES),
        sibling.reshape(devices * 8, LANES),
    )

    slot_pos = jnp.arange(cap, dtype=jnp.int32)
    live = (slot_pos[None, :] < fill_counts[0][:, None]).astype(jnp.int32).reshape(1, slots)
    coded, best = pl.pallas_call(
        score_kernel,
        grid=(steps,),
        in_specs=[
            pl.BlockSpec((LANES, slots), lambda i: (i, 0)),
            pl.BlockSpec((LANES, slots), lambda i: (i, 0)),
            pl.BlockSpec((slots, LANES), lambda i: (0, i)),
            pl.BlockSpec((per, 256, LANES), lambda i: (i, 0, 0)),
            pl.BlockSpec((1, slots), lambda i: (0, 0)),
        ],
        out_specs=[pl.BlockSpec((1, slots), lambda i: (0, 0))] * 2,
        out_shape=[jax.ShapeDtypeStruct((1, slots), f32)] * 2,
        scratch_shapes=[pltpu.VMEM((24, slots), f32)],
        name="score",
    )(vt, wt, cent, a, live)
    return coded.reshape(slots), best.reshape(slots)


def solution(mesh):
    in_specs = (
        P(BOTH, None),
        P(BOTH),
        P(BOTH, None),
        P(BOTH, None),
        P(BOTH, None),
        P("col", None, None),
    )
    out_specs = (P(BOTH), P(BOTH))
    return jax.shard_map(local, mesh=mesh, in_specs=in_specs, out_specs=out_specs, check_vma=False)
```

time: 406 us -> 96.9 us (0.24)
  matrix products: 159 us -> 0 us
  local copies, waits for them, and re-layouts: 118 us -> 8.61 us
  other arithmetic: 59 us -> 0.49 us
  blocking collectives: 60.1 us -> 25.1 us
  waiting for transfers between devices: 0.36 us -> 27.7 us
  Pallas kernels: 0 us -> 27 us
    dot_general x8 -> x0, matrix products: 159 us -> none  [block_terms(): jnp.einsum('bms,msk->bmk', block_vec, shard_piece, precision=lax.Precisio...]
    sub x1 -> x0, other arithmetic: 49.1 us -> none  [local(): got_vec - jnp.take(centroids, got_ids % centroids.shape[0], axis=0)]
    while x2 -> x0, local copies, waits for them, and re-layouts: 36.3 us -> none  [local(): parts = lax.map(one_block, (shaped, shaped_codes))]
    all_to_all x3 -> x1, blocking collectives: 60.1 us -> 25.1 us  [local(): got = lax.all_to_all(sent, BOTH, 0, 0, tiled=True)]
    reshape x3 -> x1, local copies, waits for them, and re-layouts: 32.4 us -> 0.77 us  [local(): ids = (list_ids.reshape(devices, 1, cap) % centroids.shape[0]).astype(f32)]
    gather x2 -> x1, local copies, waits for them, and re-layouts: 36.3 us -> 5.26 us  [local(): picked = centroids.at[want].get(mode='promise_in_bounds')]
    pallas_call x0 -> x2, Pallas kernels: none -> 27 us  [the longest x1 17.1 us: local(): pl.pallas_call(score_kernel, grid=(steps,), in_specs=[pl.BlockSpec((LANES...]
    all_to_all x1, waiting for transfers between devices: 0.36 us -> 27 us  [local(): lax.all_to_all(picked.reshape(devices, cap, width), BOTH, 0, 0, tiled=True)]
  transfers between devices with their start and end apart: 1 -> 2, of which waited for: 1 -> 2; matrix products, arithmetic and copies ran while one was open for 10% -> 1% of each run, Pallas kernels for 0% -> 10%
where the time goes in v1:
time: 96.9 us; the launch traced here: 96.5 us
  waiting for transfers between devices  27.7 us (29%)
  Pallas kernels  27 us (28%)
  blocking collectives  25.1 us (26%)
  local copies, waits for them, and re-layouts  8.61 us (9%)
  starting transfers between devices  6.74 us (7%)
    all_to_all x1, waiting for transfers between devices, local(): lax.all_to_all(picked.reshape(devices, cap, width), BOTH, 0, 0, tiled=True)  27 us
    all_to_all x1, blocking collectives, local(): got = lax.all_to_all(sent, BOTH, 0, 0, tiled=True)  25.1 us
    pallas_call x1, Pallas kernels, local(): pl.pallas_call(score_kernel, grid=(steps,), in_specs=[pl.BlockSpec((LANES...  17.1 us
    pallas_call x1, Pallas kernels, local(): pl.pallas_call(prep_kernel, grid=(steps,), in_specs=[pl.BlockSpec(memory_...  9.88 us
    all_to_all x1, starting transfers between devices, local(): lax.all_to_all(picked.reshape(devices, cap, width), BOTH, 0, 0, tiled=True)  5.39 us
    gather x1, local copies, waits for them, and re-layouts, local(): picked = centroids.at[want].get(mode='promise_in_bounds')  5.26 us
  transfers between devices with their start and end apart: 2, of which 2 were waited for; matrix products, arithmetic and copies ran while one was open for 1% of the time, Pallas kernels for 10%

profile of v1, /device:TPU:1, one launch (start us, length us, event | category | flops | bytes accessed | tf_op | source)
XLA Modules:
  0.0 96.5 jit_solution(11019110212514492677)
XLA Ops:
  0.6 0.0 copy-start
  0.6 0.9 dynamic-slice_reduce_fusion
  1.6 0.8 reshape.149
  2.5 0.1 select_maximum_fusion
  2.6 25.1 %all_to_all.10 = f32[128,8,128]{2,1,0:T(8,128)S(1)} all-to-all(f32[128,8,128]{2,1,0:T(8,128)S(1)} %select_maximum_fusion), channel_id=1, replica_groups=mesh['row'=8,'col'=16] {'row','col'}, dimensions={0} | all-to-all | bytes 1048576 | tf_op jit(solution)/shard_map/all_to_all | solution.py:128
  27.8 0.0 copy-start.1
  27.8 0.2 fusion.2
  28.0 0.1 convert_element_type.42
  28.1 0.0 copy-done
  28.1 5.3 %gather_fusion = f32[1024,768]{1,0:T(8,128)} fusion(f32[512,768]{1,0:T(8,128)S(1)} %copy-done, s32[1024]{0:T(1024)S(1)} %broadcast_clamp_fusion), kind=kCustom, calls=%fused_computation | custom fusion | bytes 6295552 | tf_op jit(solution)/shard_map/gather | solution.py:132
  33.4 0.0 copy-start.3
  33.4 5.4 %all-to-all-start.1 = ((f32[128,8,768]{2,1,0:T(8,128)}), f32[128,8,768]{2,1,0:T(8,128)}, u32[]{:S(2)}, u32[]{:S(2)}) async-start(f32[128,8,768]{2,1,0:T(8,128)} %bitcast.12), calls=%async_computation.1 | async-start | bytes 6291456 | tf_op jit(solution)/shard_map/all_to_all | solution.py:133
  38.8 0.0 copy-done.1
  38.8 1.4 %collective-permute-start = (f32[128,8,128]{2,1,0:T(8,128)S(1)}, f32[128,8,128]{2,1,0:T(8,128)S(1)}, u32[]{:S(2)}, u32[]{:S(2)}) collective-permute-start(f32[128,8,128]{2,1,0:T(8,128)S(1)} %all_to_all.10), channel_id=1, source_target_pairs={{0,16},{16,0},{32,48},{48,32},{64,80},{80,64},{96,112},{112,96},{1... | collective-permute-start | bytes 1572872 | tf_op jit(solution)/shard_map/ppermute | solution.py:129
  40.1 0.0 copy-done.3
  40.1 0.1 fusion.3
  40.2 0.7 reshape.156.live_ref
  40.9 0.8 collective-permute-done
  41.7 0.0 copy-start.2
  41.7 0.8 copy-done.2
  42.5 9.9 %prep.1 = (f32[768,1024]{1,0:T(8,128)}, f32[768,1024]{1,0:T(8,128)}, bf16[96,256,128]{2,1,0:T(8,128)(2,1)}) custom-call(s32[1]{0:T(128)} %bitcast.core_ref, f32[1024,768]{1,0:T(8,128)} %vec_ref.1, s32[96,1024]{1,0:T(8,128)} %bitcast.16, f32[1024,128]{1,0:T(8,128)} %bitcast.13, f32[1024,128]{1,0:T(8,128)} %bitcast.15), custom_call_target="tpu_custom_call" | custom-call | tf_op jit(solution)/shard_map/prep/pallas_call | solution.py:138
  52.4 27.0 %all-to-all-done.1 = f32[128,8,768]{2,1,0:T(8,128)} async-done(((f32[128,8,768]{2,1,0:T(8,128)}), f32[128,8,768]{2,1,0:T(8,128)}, u32[]{:S(2)}, u32[]{:S(2)}) %all-to-all-start.1) | async-done | bytes 3145760 | tf_op jit(solution)/shard_map/all_to_all | solution.py:133
  79.3 17.1 %score.1 = (f32[1,1024]{1,0:T(1,128)}, f32[1,1024]{1,0:T(1,128)}) custom-call(f32[768,1024]{1,0:T(8,128)} %get-tuple-element.7.vt_ref, f32[768,1024]{1,0:T(8,128)} %get-tuple-element.8.wt_ref, f32[1024,768]{1,0:T(8,128)} %bitcast.7.cent_ref, bf16[96,256,128]{2,1,0:T(8,128)(2,1)} %get-tuple-element.9.a_ref, s32[1,1024]{1,0:T(1,128)} %reshape.156.live_ref), custom_call_target="tpu_custom_call" | custom-call | tf_op jit(solution)/shard_map/score/pallas_call | solution.py:169
  (5 shorter events, 0.1 us)
Async XLA Ops:
  0.6 27.5 %copy-start = (f32[512,768]{1,0:T(8,128)S(1)}, f32[512,768]{1,0:T(8,128)}, u32[]{:S(2)}) copy-start(f32[512,768]{1,0:T(8,128)} %param.10) | copy-start | bytes 4718596
  27.8 11.0 %copy-start.1 = (f32[128,8,128]{2,1,0:T(8,128)}, f32[128,8,128]{2,1,0:T(8,128)S(1)}, u32[]{:S(2)}) copy-start(f32[128,8,128]{2,1,0:T(8,128)S(1)} %all_to_all.10) | copy-start | bytes 1572868
  33.4 6.8 %copy-start.3 = (s32[1,128]{1,0:T(1,128)S(1)}, s32[1,128]{1,0:T(1,128)}, u32[]{:S(2)}) copy-start(s32[1,128]{1,0:T(1,128)} %param.9) | copy-start | bytes 1540
  33.4 46.0 %all-to-all-start.1 = ((f32[128,8,768]{2,1,0:T(8,128)}), f32[128,8,768]{2,1,0:T(8,128)}, u32[]{:S(2)}, u32[]{:S(2)}) async-start(f32[128,8,768]{2,1,0:T(8,128)} %bitcast.12), calls=%async_computation.1 | async-start | bytes 6291456 | tf_op jit(solution)/shard_map/all_to_all | solution.py:133
  38.8 2.9 %collective-permute-start = (f32[128,8,128]{2,1,0:T(8,128)S(1)}, f32[128,8,128]{2,1,0:T(8,128)S(1)}, u32[]{:S(2)}, u32[]{:S(2)}) collective-permute-start(f32[128,8,128]{2,1,0:T(8,128)S(1)} %all_to_all.10), channel_id=1, source_target_pairs={{0,16},{16,0},{32,48},{48,32},{64,80},{80,64},{96,112},{112,96},{1... | collective-permute-start | bytes 1572872 | tf_op jit(solution)/shard_map/ppermute | solution.py:129
  41.7 0.8 copy-start.2

commit v2 on v1

v2 whole, which is shorter than its diff:
```python
import jax
import jax.numpy as jnp
from jax import lax
from jax.experimental import pallas as pl
from jax.experimental.pallas import tpu as pltpu
from jax.sharding import PartitionSpec as P

BOTH = ("row", "col")
LANES = 128
SPLITS = 64


def three_way(x):
    hi = x.astype(jnp.bfloat16).astype(jnp.float32)
    rest = x - hi
    mid = rest.astype(jnp.bfloat16).astype(jnp.float32)
    lo = (rest - mid).astype(jnp.bfloat16).astype(jnp.float32)
    return hi, mid, lo


def prep_kernel(core_ref, vec_ref, codes_ref, own_ref, sib_ref, vt_ref, wt_ref, a_ref):
    core = core_ref[0]
    rows, width = vec_ref.shape
    sublane = lax.broadcasted_iota(jnp.int32, (8, 256), 0)
    for block in range(width // LANES):
        for g in range(rows // LANES):
            vt_ref[block * LANES : (block + 1) * LANES, g * LANES : (g + 1) * LANES] = vec_ref[
                g * LANES : (g + 1) * LANES, block * LANES : (block + 1) * LANES
            ].T

    def some_subspaces(step, carry):
        codes = codes_ref[pl.ds(pl.multiple_of(step * 8, 8), 8), :]
        stack = []
        for i in range(8):
            m = step * 8 + i
            shard, within = m // 6, m % 6
            half, j = within // 3, within % 3
            base = shard * 8 + j * 2
            mine = half == core
            words = []
            for h in range(2):
                spot = pl.ds(base + h, 8, stride=LANES)
                words.append(jnp.where(mine, own_ref[spot, :], sib_ref[spot, :]))
            at = pl.ds(pl.multiple_of(m * 8, 8), 8)
            for g in range(rows // LANES):
                cut = slice(g * LANES, (g + 1) * LANES)
                code = jnp.broadcast_to(codes[i : i + 1, cut], (8, LANES))
                low = code & (LANES - 1)
                first = jnp.take_along_axis(words[0], low, axis=1, mode="promise_in_bounds")
                second = jnp.take_along_axis(words[1], low, axis=1, mode="promise_in_bounds")
                wt_ref[at, cut] = vt_ref[at, cut] - jnp.where(code >= LANES, second, first)
            both = jnp.concatenate(words, axis=1)
            norm = jnp.sum(both * both, axis=0, keepdims=True)
            hi, mid, lo = three_way(-2.0 * both)
            nhi, nmid, nlo = three_way(norm)
            norms = jnp.where(sublane == 0, nhi, jnp.where(sublane == 1, nmid, jnp.where(sublane == 2, nlo, 0.0)))
            stack += [hi, hi, hi, mid, mid, lo, norms, jnp.zeros_like(norms)]
            if i % 2 == 1:
                a_ref[m // 2] = jnp.concatenate(stack, axis=0).T.astype(jnp.bfloat16)
                stack = []
        return carry

    lax.fori_loop(0, codes_ref.shape[0] // 8, some_subspaces, 0)


PARTS = 8


def pick_kernel(start_ref, cent_ref, out_hbm, out_ref, sems):
    tiles = 6
    words = out_ref.shape[0] // PARTS
    slots = words // tiles
    copies = []
    for part in range(PARTS):

        def some(i, carry, part=part):
            for k in range(32):
                row = cent_ref[pl.ds(start_ref[part * slots + i * 32 + k], tiles, stride=8), :]
                out_ref[pl.ds(part * words + (i * 4 + k // 8) * (8 * tiles) + k % 8, tiles, stride=8), :] = row
            return carry

        lax.fori_loop(0, slots // 32, some, 0)
        cut = slice(part * words, (part + 1) * words)
        copies.append(pltpu.make_async_copy(out_ref.at[cut], out_hbm.at[cut], sems.at[part]))
        copies[-1].start()
    for copy in copies:
        copy.wait()


def tiled_view(x):
    n, w = x.shape
    return x.reshape(n // 8, 8, w // LANES, LANES).swapaxes(1, 2).reshape(n * w // LANES, LANES)


def untiled_view(x, n, w):
    return x.reshape(n // 8, w // LANES, 8, LANES).swapaxes(1, 2).reshape(n, w)


STAGES = ((0, 1), (1, 3), (3, 6))


def score_kernel(vt_hbm, wt_hbm, cent_ref, a_hbm, live_ref, coded_ref, best_ref, vt_ref, wt_ref, a_ref, acc_ref, sems):
    rows, width = cent_ref.shape
    wide = 256
    tiles = rows // wide
    copies = []
    for k, (lo, hi) in enumerate(STAGES):
        pairs = slice(lo * 8, hi * 8)
        feats = slice(lo * LANES, hi * LANES)
        copies.append(
            [
                pltpu.make_async_copy(a_hbm.at[pairs], a_ref.at[pairs], sems.at[k, 0]),
                pltpu.make_async_copy(vt_hbm.at[feats], vt_ref.at[feats], sems.at[k, 1]),
                pltpu.make_async_copy(wt_hbm.at[feats], wt_ref.at[feats], sems.at[k, 2]),
            ]
        )
        for copy in copies[-1]:
            copy.start()
    acc_ref[...] = jnp.zeros_like(acc_ref)
    ones = jnp.ones((16, wide), jnp.bfloat16)
    none = jnp.zeros((SPLITS, wide), jnp.bfloat16)
    for k, (lo, hi) in enumerate(STAGES):
        for copy in copies[k]:
            copy.wait()
        for block in range(lo, hi):
            feats = slice(block * LANES, (block + 1) * LANES)
            for t in range(tiles):
                cut = slice(t * wide, (t + 1) * wide)
                turned = jnp.concatenate(
                    [
                        cent_ref[t * wide + g * LANES : t * wide + (g + 1) * LANES, feats].T
                        for g in range(wide // LANES)
                    ],
                    axis=1,
                )
                resid = vt_ref[feats, cut] - turned
                err = wt_ref[feats, cut] - turned
                least = jnp.zeros((1, wide), jnp.float32)
                for pair in range(8):
                    left = a_ref[block * 8 + pair]
                    for half in range(2):
                        at = (pair * 2 + half) * 8
                        hi_, mid, low = three_way(resid[at : at + 8, :])
                        side = [
                            jnp.concatenate([hi_, mid], axis=0).astype(jnp.bfloat16),
                            jnp.concatenate([low, hi_], axis=0).astype(jnp.bfloat16),
                            jnp.concatenate([mid, hi_], axis=0).astype(jnp.bfloat16),
                            ones,
                        ]
                        side = [none] + side if half else side + [none]
                        table = jnp.dot(left, jnp.concatenate(side, axis=0), preferred_element_type=jnp.float32)
                        least += jnp.min(table, axis=0, keepdims=True)
                acc_ref[0:8, cut] += jnp.sum((err * err).reshape(16, 8, wide), axis=0)
                acc_ref[8:16, cut] += jnp.sum((resid * resid).reshape(16, 8, wide), axis=0)
                acc_ref[16:17, cut] += least
    live = live_ref[...] != 0
    coded = jnp.sum(acc_ref[0:8, :], axis=0, keepdims=True)
    best = jnp.sum(acc_ref[8:16, :], axis=0, keepdims=True) + acc_ref[16:17, :]
    coded_ref[...] = jnp.where(live, coded, 0.0)
    best_ref[...] = jnp.where(live, best, 0.0)


def pinned(x):
    return pltpu.with_memory_space_constraint(x, pltpu.HBM)


def local(vectors, list_ids, pq_codes, fill_counts, centroids, codebook):
    row_count = lax.axis_size("row")
    col_count = lax.axis_size("col")
    devices = row_count * col_count
    slots, width = vectors.shape
    cap = slots // devices
    subs = pq_codes.shape[1]
    f32 = jnp.float32
    my_row = lax.axis_index("row")
    core = my_row % 2

    coord = lax.dynamic_index_in_dim(codebook, my_row, axis=1, keepdims=False)
    halves = coord.reshape(2, 6, LANES)
    piece = jnp.broadcast_to(halves[None, :, None], (row_count // 2, 2, col_count, 6, LANES))
    piece = piece.reshape(devices, 6, LANES)
    per_row = LANES // cap
    ids = list_ids.astype(f32).reshape(devices // per_row, 1, 1, LANES)
    ids = jnp.broadcast_to(ids, (devices // per_row, per_row, 2, LANES)).reshape(devices, 2, LANES)
    sent = jnp.concatenate([piece, ids], axis=1)
    got = lax.all_to_all(sent, BOTH, 0, 0, tiled=True)
    sibling = lax.ppermute(got, "row", [(i, i ^ 1) for i in range(row_count)])

    me = my_row * col_count + lax.axis_index("col")
    want = lax.dynamic_slice(got[:, 6], (0, (me % per_row) * cap), (devices, cap))
    want = want.astype(jnp.int32).reshape(slots) % centroids.shape[0]
    start = (want // 8) * (8 * width // LANES) + want % 8
    vmem = pl.BlockSpec(memory_space=pltpu.VMEM)
    smem = pl.BlockSpec(memory_space=pltpu.SMEM)
    hbm = pl.BlockSpec(memory_space=pltpu.HBM)
    picked = pl.pallas_call(
        pick_kernel,
        in_specs=[smem, vmem],
        out_specs=hbm,
        out_shape=pltpu.HBM((slots * width // LANES, LANES), f32),
        scratch_shapes=[pltpu.VMEM((slots * width // LANES, LANES), f32), pltpu.SemaphoreType.DMA((PARTS,))],
        compiler_params=pltpu.CompilerParams(vmem_limit_bytes=8 << 20),
        name="pick",
    )(start, tiled_view(centroids))
    picked = untiled_view(picked, slots, width)
    cent = lax.all_to_all(picked.reshape(devices, cap, width), BOTH, 0, 0, tiled=True)
    cent = cent.reshape(slots, width)

    vt, wt, a = pl.pallas_call(
        prep_kernel,
        in_specs=[smem, vmem, vmem, vmem, vmem],
        out_specs=[vmem] * 3,
        out_shape=[
            jax.ShapeDtypeStruct((width, slots), f32),
            jax.ShapeDtypeStruct((width, slots), f32),
            jax.ShapeDtypeStruct((subs // 2, 256, LANES), jnp.bfloat16),
        ],
        compiler_params=pltpu.CompilerParams(vmem_limit_bytes=24 << 20),
        name="prep",
    )(
        core.reshape(1).astype(jnp.int32),
        vectors,
        pq_codes.T,
        got.reshape(devices * 8, LANES),
        sibling.reshape(devices * 8, LANES),
    )

    slot_pos = jnp.arange(cap, dtype=jnp.int32)
    live = (slot_pos[None, :] < fill_counts[0][:, None]).astype(jnp.int32).reshape(1, slots)
    coded, best = pl.pallas_call(
        score_kernel,
        in_specs=[hbm, hbm, vmem, hbm, vmem],
        out_specs=[vmem] * 2,
        out_shape=[jax.ShapeDtypeStruct((1, slots), f32)] * 2,
        scratch_shapes=[
            pltpu.VMEM((width, slots), f32),
            pltpu.VMEM((width, slots), f32),
            pltpu.VMEM((subs // 2, 256, LANES), jnp.bfloat16),
            pltpu.VMEM((24, slots), f32),
            pltpu.SemaphoreType.DMA((len(STAGES), 3)),
        ],
        compiler_params=pltpu.CompilerParams(vmem_limit_bytes=32 << 20),
        name="score",
    )(pinned(vt), pinned(wt), cent, pinned(a), live)
    return coded.reshape(slots), best.reshape(slots)


def solution(mesh):
    in_specs = (
        P(BOTH, None),
        P(BOTH),
        P(BOTH, None),
        P(BOTH, None),
        P(BOTH, None),
        P("col", None, None),
    )
    out_specs = (P(BOTH), P(BOTH))
    return jax.shard_map(local, mesh=mesh, in_specs=in_specs, out_specs=out_specs, check_vma=False)
```

time: 96.9 us -> 93.1 us (0.961)
  blocking collectives: 25.1 us -> 0 us
  starting transfers between devices: 6.74 us -> 17 us
  waiting for transfers between devices: 27.7 us -> 36.4 us
  other arithmetic: 0.49 us -> 2.07 us
    all_to_all x1 -> x0, blocking collectives: 25.1 us -> none  [local(): got = lax.all_to_all(sent, BOTH, 0, 0, tiled=True)]
    all_to_all x0 -> x1, waiting for transfers between devices: none -> 13.8 us  [local(): got = lax.all_to_all(sent, BOTH, 0, 0, tiled=True)]
    all_to_all x0 -> x1, starting transfers between devices: none -> 11.5 us  [local(): got = lax.all_to_all(sent, BOTH, 0, 0, tiled=True)]
    unnamed x8 -> x20, local copies, waits for them, and re-layouts: 0.84 us -> 8.98 us
    all_to_all x1, waiting for transfers between devices: 27 us -> 20.9 us  [local(): lax.all_to_all(picked.reshape(devices, cap, width), BOTH, 0, 0, tiled=True)]
    gather x1 -> x0, local copies, waits for them, and re-layouts: 5.26 us -> none  [local(): picked = centroids.at[want].get(mode='promise_in_bounds')]
    all_to_all x1, starting transfers between devices: 5.39 us -> 4.28 us  [local(): lax.all_to_all(picked.reshape(devices, cap, width), BOTH, 0, 0, tiled=True)]
    pallas_call x2 -> x3, Pallas kernels: 27 us -> 26.8 us  [the longest x1 16 us: local(): pl.pallas_call(score_kernel, in_specs=[hbm, hbm, vmem, hbm, vmem], out_sp...]
  transfers between devices with their start and end apart: 2 -> 3, of which waited for: 2 -> 3; matrix products, arithmetic and copies ran while one was open for 1% -> 0% of each run, Pallas kernels for 10% -> 8%
where the time goes in v2:
time: 93.1 us; the launch traced here: 92.7 us
  waiting for transfers between devices  36.4 us (39%)
  Pallas kernels  26.8 us (29%)
  starting transfers between devices  17 us (18%)
  local copies, waits for them, and re-layouts  9.34 us (10%)
  other arithmetic  2.07 us (2%)
  between operations  0.97 us (1%)
    all_to_all x1, waiting for transfers between devices, local(): lax.all_to_all(picked.reshape(devices, cap, width), BOTH, 0, 0, tiled=True)  20.9 us
    pallas_call x1, Pallas kernels, local(): pl.pallas_call(score_kernel, in_specs=[hbm, hbm, vmem, hbm, vmem], out_sp...  16 us
    all_to_all x1, waiting for transfers between devices, local(): got = lax.all_to_all(sent, BOTH, 0, 0, tiled=True)  13.8 us
    all_to_all x1, starting transfers between devices, local(): got = lax.all_to_all(sent, BOTH, 0, 0, tiled=True)  11.5 us
    unnamed x20, local copies, waits for them, and re-layouts  8.98 us
    pallas_call x1, Pallas kernels, local(): pl.pallas_call(prep_kernel, in_specs=[smem, vmem, vmem, vmem, vmem], out_...  7.8 us
    all_to_all x1, starting transfers between devices, local(): lax.all_to_all(picked.reshape(devices, cap, width), BOTH, 0, 0, tiled=True)  4.28 us
    pallas_call x1, Pallas kernels, local(): pl.pallas_call(pick_kernel, in_specs=[smem, vmem], out_specs=hbm, out_sha...  3.03 us
  transfers between devices with their start and end apart: 3, of which 3 were waited for; matrix products, arithmetic and copies ran while one was open for 0% of the time, Pallas kernels for 8%

profile of v2, /device:TPU:1, one launch (start us, length us, event | category | flops | bytes accessed | tf_op | source)
XLA Modules:
  0.0 92.7 jit_solution(14360521457217860805)
XLA Ops:
  0.6 0.0 copy-start
  0.7 0.8 convert_bitcast_fusion
  1.6 0.9 pad_maximum_fusion
  2.5 11.5 %all-to-all-start = ((f32[128,8,128]{2,1,0:T(8,128)}), f32[128,8,128]{2,1,0:T(8,128)S(1)}, u32[]{:S(2)}, u32[]{:S(2)}) async-start(f32[128,8,128]{2,1,0:T(8,128)} %pad_maximum_fusion), calls=%async_computation | async-start | bytes 1048576 | tf_op jit(solution)/shard_map/all_to_all | solution.py:186
  14.0 13.8 %all-to-all-done = f32[128,8,128]{2,1,0:T(8,128)S(1)} async-done(((f32[128,8,128]{2,1,0:T(8,128)}), f32[128,8,128]{2,1,0:T(8,128)S(1)}, u32[]{:S(2)}, u32[]{:S(2)}) %all-to-all-start) | async-done | bytes 524320 | tf_op jit(solution)/shard_map/all_to_all | solution.py:186
  27.9 0.1 slice.4
  27.9 0.3 convert_reduce_fusion
  28.2 0.1 convert_element_type.25
  28.3 3.0 %pick.1 = f32[6144,128]{1,0:T(8,128)} custom-call(s32[1024]{0:T(1024)S(1)} %fusion.3.start_ref, f32[3072,128]{1,0:T(8,128)S(1)} %bitcast.24), custom_call_target="tpu_custom_call" | custom-call | tf_op jit(solution)/shard_map/pick/pallas_call | solution.py:196
  31.4 0.0 copy-start.9
  31.4 4.3 %all-to-all-start.1 = ((f32[128,8,768]{2,1,0:T(8,128)}), f32[128,8,768]{2,1,0:T(8,128)S(1)}, u32[]{:S(2)}, u32[]{:S(2)}) async-start(f32[128,8,768]{2,1,0:T(8,128)} %bitcast.26), calls=%async_computation.1 | async-start | bytes 6291456 | tf_op jit(solution)/shard_map/all_to_all | solution.py:206
  35.7 1.3 %collective-permute-start = (f32[128,8,128]{2,1,0:T(8,128)}, f32[128,8,128]{2,1,0:T(8,128)}, u32[]{:S(2)}, u32[]{:S(2)}) collective-permute-start(f32[128,8,128]{2,1,0:T(8,128)} %copy-done.5), channel_id=1, source_target_pairs={{0,16},{16,0},{32,48},{48,32},{64,80},{80,64},{96,112},{112,96},{1... | collective-permute-start | bytes 1572872 | tf_op jit(solution)/shard_map/ppermute | solution.py:187
  37.0 0.1 fusion
  37.0 0.1 reshape.83.live_ref
  37.1 1.7 %collective-permute-done = f32[128,8,128]{2,1,0:T(8,128)} collective-permute-done((f32[128,8,128]{2,1,0:T(8,128)}, f32[128,8,128]{2,1,0:T(8,128)}, u32[]{:S(2)}, u32[]{:S(2)}) %collective-permute-start) | collective-permute-done | bytes 524320 | tf_op jit(solution)/shard_map/ppermute | solution.py:187
  38.8 1.9 %copy-done.1 = f32[1024,768]{1,0:T(8,128)S(1)} copy-done((f32[1024,768]{1,0:T(8,128)S(1)}, f32[1024,768]{1,0:T(8,128)}, u32[]{:S(2)}) %copy-start.1) | copy-done | bytes 3145752
  40.7 1.0 %copy-done.6 = f32[128,8,128]{2,1,0:T(8,128)S(1)} copy-done((f32[128,8,128]{2,1,0:T(8,128)S(1)}, f32[128,8,128]{2,1,0:T(8,128)}, u32[]{:S(2)}) %copy-start.6) | copy-done | bytes 524312
  41.8 1.0 %copy-done.8 = s32[1024,96]{0,1:T(8,128)S(1)} copy-done((s32[1024,96]{0,1:T(8,128)S(1)}, s32[1024,96]{0,1:T(8,128)}, u32[]{:S(2)}) %copy-start.8) | copy-done | bytes 393240
  42.8 7.8 %prep.1 = (f32[768,1024]{1,0:T(8,128)S(1)}, f32[768,1024]{1,0:T(8,128)S(1)}, bf16[48,256,128]{2,1,0:T(8,128)(2,1)S(1)}) custom-call(s32[1]{0:T(128)} %bitcast.core_ref, f32[1024,768]{1,0:T(8,128)S(1)} %copy-done.1, s32[96,1024]{1,0:T(8,128)S(1)} %bitcast.25, f32[1024,128]{1,0:T(8,128)S(1)} %bitcast.23, f32[1024,128]{1,0:T(8,128)} %bitcast.6.sib_ref), custom_call_target="tpu_custom_call" | custom-call | tf_op jit(solution)/shard_map/prep/pallas_call | solution.py:209
  50.6 1.7 %copy-done.2 = f32[768,1024]{1,0:T(8,128)} copy-done((f32[768,1024]{1,0:T(8,128)}, f32[768,1024]{1,0:T(8,128)S(1)}, u32[]{:S(2)}) %copy-start.2) | copy-done | bytes 3145752
  52.2 1.7 %copy-done.3 = f32[768,1024]{1,0:T(8,128)} copy-done((f32[768,1024]{1,0:T(8,128)}, f32[768,1024]{1,0:T(8,128)S(1)}, u32[]{:S(2)}) %copy-start.3) | copy-done | bytes 3145752
  54.0 1.6 %copy-done.4 = bf16[48,256,128]{2,1,0:T(8,128)(2,1)} copy-done((bf16[48,256,128]{2,1,0:T(8,128)(2,1)}, bf16[48,256,128]{2,1,0:T(8,128)(2,1)S(1)}, u32[]{:S(2)}) %copy-start.4) | copy-done | bytes 3145752
  55.6 20.9 %all-to-all-done.1 = f32[128,8,768]{2,1,0:T(8,128)S(1)} async-done(((f32[128,8,768]{2,1,0:T(8,128)}), f32[128,8,768]{2,1,0:T(8,128)S(1)}, u32[]{:S(2)}, u32[]{:S(2)}) %all-to-all-start.1) | async-done | bytes 3145760 | tf_op jit(solution)/shard_map/all_to_all | solution.py:206
  76.5 16.0 %score.1 = (f32[1,1024]{1,0:T(1,128)}, f32[1,1024]{1,0:T(1,128)}) custom-call(f32[768,1024]{1,0:T(8,128)} %copy-done.2, f32[768,1024]{1,0:T(8,128)} %copy-done.3, f32[1024,768]{1,0:T(8,128)S(1)} %bitcast.22, bf16[48,256,128]{2,1,0:T(8,128)(2,1)} %copy-done.4, s32[1,1024]{1,0:T(1,128)S(1)} %reshape.83.live_ref), custom_call_target="tpu_custom_call" | custom-call | tf_op jit(solution)/shard_map/score/pallas_call | solution.py:230
  (18 shorter events, 0.2 us)
Async XLA Ops:
  0.6 0.8 copy-start
  0.6 27.7 %copy-start.7 = (f32[512,768]{1,0:T(8,128)S(1)}, f32[512,768]{1,0:T(8,128)}, u32[]{:S(2)}) copy-start(f32[512,768]{1,0:T(8,128)} %param.10) | copy-start | bytes 4718596
  2.5 25.3 %all-to-all-start = ((f32[128,8,128]{2,1,0:T(8,128)}), f32[128,8,128]{2,1,0:T(8,128)S(1)}, u32[]{:S(2)}, u32[]{:S(2)}) async-start(f32[128,8,128]{2,1,0:T(8,128)} %pad_maximum_fusion), calls=%async_computation | async-start | bytes 1048576 | tf_op jit(solution)/shard_map/all_to_all | solution.py:186
  27.9 3.5 %copy-start.5 = (f32[128,8,128]{2,1,0:T(8,128)}, f32[128,8,128]{2,1,0:T(8,128)S(1)}, u32[]{:S(2)}) copy-start(f32[128,8,128]{2,1,0:T(8,128)S(1)} %all-to-all-done) | copy-start | bytes 1572868
  31.4 5.6 %copy-start.9 = (s32[1,128]{1,0:T(1,128)S(1)}, s32[1,128]{1,0:T(1,128)}, u32[]{:S(2)}) copy-start(s32[1,128]{1,0:T(1,128)} %param.9) | copy-start | bytes 1540
  31.4 45.1 %all-to-all-start.1 = ((f32[128,8,768]{2,1,0:T(8,128)}), f32[128,8,768]{2,1,0:T(8,128)S(1)}, u32[]{:S(2)}, u32[]{:S(2)}) async-start(f32[128,8,768]{2,1,0:T(8,128)} %bitcast.26), calls=%async_computation.1 | async-start | bytes 6291456 | tf_op jit(solution)/shard_map/all_to_all | solution.py:206
  35.7 3.2 %collective-permute-start = (f32[128,8,128]{2,1,0:T(8,128)}, f32[128,8,128]{2,1,0:T(8,128)}, u32[]{:S(2)}, u32[]{:S(2)}) collective-permute-start(f32[128,8,128]{2,1,0:T(8,128)} %copy-done.5), channel_id=1, source_target_pairs={{0,16},{16,0},{32,48},{48,32},{64,80},{80,64},{96,112},{112,96},{1... | collective-permute-start | bytes 1572872 | tf_op jit(solution)/shard_map/ppermute | solution.py:187
  38.8 1.9 %copy-start.1 = (f32[1024,768]{1,0:T(8,128)S(1)}, f32[1024,768]{1,0:T(8,128)}, u32[]{:S(2)}) copy-start(f32[1024,768]{1,0:T(8,128)} %vec_ref.1) | copy-start | bytes 9437188
  40.7 1.0 %copy-start.6 = (f32[128,8,128]{2,1,0:T(8,128)S(1)}, f32[128,8,128]{2,1,0:T(8,128)}, u32[]{:S(2)}) copy-start(f32[128,8,128]{2,1,0:T(8,128)} %copy-done.5) | copy-start | bytes 1572868
  41.8 1.0 %copy-start.8 = (s32[1024,96]{0,1:T(8,128)S(1)}, s32[1024,96]{0,1:T(8,128)}, u32[]{:S(2)}) copy-start(s32[1024,96]{0,1:T(8,128)} %param.8) | copy-start | bytes 1179652
  50.6 1.7 %copy-start.2 = (f32[768,1024]{1,0:T(8,128)}, f32[768,1024]{1,0:T(8,128)S(1)}, u32[]{:S(2)}) copy-start(f32[768,1024]{1,0:T(8,128)S(1)} %get-tuple-element.7.vt_hbm) | copy-start | bytes 9437188
  52.2 1.7 %copy-start.3 = (f32[768,1024]{1,0:T(8,128)}, f32[768,1024]{1,0:T(8,128)S(1)}, u32[]{:S(2)}) copy-start(f32[768,1024]{1,0:T(8,128)S(1)} %get-tuple-element.8.wt_hbm) | copy-start | bytes 9437188
  54.0 1.6 %copy-start.4 = (bf16[48,256,128]{2,1,0:T(8,128)(2,1)}, bf16[48,256,128]{2,1,0:T(8,128)(2,1)S(1)}, u32[]{:S(2)}) copy-start(bf16[48,256,128]{2,1,0:T(8,128)(2,1)S(1)} %get-tuple-element.9.a_hbm) | copy-start | bytes 9437188

commit v3 on v2

--- a/solution.py
+++ b/solution.py
@@ -18,8 +18,7 @@
     return hi, mid, lo
 
 
-def prep_kernel(core_ref, vec_ref, codes_ref, own_ref, sib_ref, vt_ref, wt_ref, a_ref):
-    core = core_ref[0]
+def prep_kernel(spot_ref, vec_ref, codes_ref, book_ref, vt_ref, wt_ref, a_ref):
     rows, width = vec_ref.shape
     sublane = lax.broadcasted_iota(jnp.int32, (8, 256), 0)
     for block in range(width // LANES):
@@ -33,14 +32,9 @@
         stack = []
         for i in range(8):
             m = step * 8 + i
-            shard, within = m // 6, m % 6
-            half, j = within // 3, within % 3
-            base = shard * 8 + j * 2
-            mine = half == core
-            words = []
-            for h in range(2):
-                spot = pl.ds(base + h, 8, stride=LANES)
-                words.append(jnp.where(mine, own_ref[spot, :], sib_ref[spot, :]))
+            at = pl.multiple_of((spot_ref[m // 6] * 6 + m % 6) * 8, 8)
+            both = book_ref[pl.ds(at, 8), :]
+            words = [both[:, :LANES], both[:, LANES:]]
             at = pl.ds(pl.multiple_of(m * 8, 8), 8)
             for g in range(rows // LANES):
                 cut = slice(g * LANES, (g + 1) * LANES)
@@ -49,7 +43,6 @@
                 first = jnp.take_along_axis(words[0], low, axis=1, mode="promise_in_bounds")
                 second = jnp.take_along_axis(words[1], low, axis=1, mode="promise_in_bounds")
                 wt_ref[at, cut] = vt_ref[at, cut] - jnp.where(code >= LANES, second, first)
-            both = jnp.concatenate(words, axis=1)
             norm = jnp.sum(both * both, axis=0, keepdims=True)
             hi, mid, lo = three_way(-2.0 * both)
             nhi, nmid, nlo = three_way(norm)
@@ -102,62 +95,102 @@
 def score_kernel(vt_hbm, wt_hbm, cent_ref, a_hbm, live_ref, coded_ref, best_ref, vt_ref, wt_ref, a_ref, acc_ref, sems):
     rows, width = cent_ref.shape
     wide = 256
-    tiles = rows // wide
-    copies = []
-    for k, (lo, hi) in enumerate(STAGES):
-        pairs = slice(lo * 8, hi * 8)
-        feats = slice(lo * LANES, hi * LANES)
-        copies.append(
-            [
-                pltpu.make_async_copy(a_hbm.at[pairs], a_ref.at[pairs], sems.at[k, 0]),
-                pltpu.make_async_copy(vt_hbm.at[feats], vt_ref.at[feats], sems.at[k, 1]),
-                pltpu.make_async_copy(wt_hbm.at[feats], wt_ref.at[feats], sems.at[k, 2]),
-            ]
-        )
-        for copy in copies[-1]:
+
+    def fetch(k):
+        lo, hi = STAGES[k]
+        pairs, feats = slice(lo * 8, hi * 8), slice(lo * LANES, hi * LANES)
+        copies = [
+            pltpu.make_async_copy(a_hbm.at[pairs], a_ref.at[pairs], sems.at[k, 0]),
+            pltpu.make_async_copy(vt_hbm.at[feats], vt_ref.at[feats], sems.at[k, 1]),
+        ]
+        if k > 0:
+            feats = slice(0 if k == 1 else lo * LANES, hi * LANES)
+            copies.append(pltpu.make_async_copy(wt_hbm.at[feats], wt_ref.at[feats], sems.at[k, 2]))
+        for copy in copies:
             copy.start()
+        return copies
+
+    def turned(block, t):
+        spots = [slice(t * wide + g * LANES, t * wide + (g + 1) * LANES) for g in range(wide // LANES)]
+        return jnp.concatenate([cent_ref[at, block * LANES : (block + 1) * LANES].T for at in spots], axis=1)
+
+    waiting = [fetch(0)]
     acc_ref[...] = jnp.zeros_like(acc_ref)
     ones = jnp.ones((16, wide), jnp.bfloat16)
     none = jnp.zeros((SPLITS, wide), jnp.bfloat16)
     for k, (lo, hi) in enumerate(STAGES):
-        for copy in copies[k]:
+        for copy in waiting[k]:
             copy.wait()
+        if k == 0:
+            waiting += [fetch(j) for j in range(1, len(STAGES))]
         for block in range(lo, hi):
             feats = slice(block * LANES, (block + 1) * LANES)
-            for t in range(tiles):
+            for t in range(rows // wide):
                 cut = slice(t * wide, (t + 1) * wide)
-                turned = jnp.concatenate(
-                    [
-                        cent_ref[t * wide + g * LANES : t * wide + (g + 1) * LANES, feats].T
-                        for g in range(wide // LANES)
-                    ],
-                    axis=1,
-                )
-                resid = vt_ref[feats, cut] - turned
-                err = wt_ref[feats, cut] - turned
+                cent = turned(block, t)
+                resid = vt_ref[feats, cut] - cent
                 least = jnp.zeros((1, wide), jnp.float32)
                 for pair in range(8):
                     left = a_ref[block * 8 + pair]
                     for half in range(2):
                         at = (pair * 2 + half) * 8
-                        hi_, mid, low = three_way(resid[at : at + 8, :])
+                        top, mid, low = three_way(resid[at : at + 8, :])
                         side = [
-                            jnp.concatenate([hi_, mid], axis=0).astype(jnp.bfloat16),
-                            jnp.concatenate([low, hi_], axis=0).astype(jnp.bfloat16),
-                            jnp.concatenate([mid, hi_], axis=0).astype(jnp.bfloat16),
+                            jnp.concatenate([top, mid], axis=0).astype(jnp.bfloat16),
+                            jnp.concatenate([low, top], axis=0).astype(jnp.bfloat16),
+                            jnp.concatenate([mid, top], axis=0).astype(jnp.bfloat16),
                             ones,
                         ]
                         side = [none] + side if half else side + [none]
                         table = jnp.dot(left, jnp.concatenate(side, axis=0), preferred_element_type=jnp.float32)
                         least += jnp.min(table, axis=0, keepdims=True)
-                acc_ref[0:8, cut] += jnp.sum((err * err).reshape(16, 8, wide), axis=0)
                 acc_ref[8:16, cut] += jnp.sum((resid * resid).reshape(16, 8, wide), axis=0)
                 acc_ref[16:17, cut] += least
+                if k > 0:
+                    err = wt_ref[feats, cut] - cent
+                    acc_ref[0:8, cut] += jnp.sum((err * err).reshape(16, 8, wide), axis=0)
+                if block == 1:
+                    err = wt_ref[0:LANES, cut] - turned(0, t)
+                    acc_ref[0:8, cut] += jnp.sum((err * err).reshape(16, 8, wide), axis=0)
     live = live_ref[...] != 0
     coded = jnp.sum(acc_ref[0:8, :], axis=0, keepdims=True)
     best = jnp.sum(acc_ref[8:16, :], axis=0, keepdims=True) + acc_ref[16:17, :]
     coded_ref[...] = jnp.where(live, coded, 0.0)
     best_ref[...] = jnp.where(live, best, 0.0)
+
+
+SIDE = 4
+
+
+def moved(x, dy, dz):
+    pairs = []
+    for y in range(SIDE):
+        for z in range(SIDE):
+            pairs.append((y * SIDE + z, (y + dy) % SIDE * SIDE + (z + dz) % SIDE))
+    return lax.ppermute(x, "col", pairs)
+
+
+def gathered_book(codebook):
+    mine = codebook.reshape(-1, codebook.shape[2])
+    with jax.named_scope("book1"):
+        back, ahead = moved(mine, 0, 1), moved(mine, 0, -1)
+    with jax.named_scope("book2"):
+        far = moved(back, 0, 1)
+    line = jnp.concatenate([mine, back, ahead, far])
+    with jax.named_scope("book3"):
+        back, ahead = moved(line, 1, 0), moved(line, -1, 0)
+    with jax.named_scope("book4"):
+        far = moved(back, 1, 0)
+    book = jnp.concatenate([line, back, ahead, far])
+    col = lax.axis_index("col")
+    shard = jnp.arange(SIDE * SIDE, dtype=jnp.int32)
+
+    def place(theirs, own):
+        ahead_by = (theirs - own) % SIDE
+        return jnp.where(ahead_by == SIDE - 1, 1, jnp.where(ahead_by == 0, 0, ahead_by + 1))
+
+    spots = place(shard // SIDE, col // SIDE) * SIDE + place(shard % SIDE, col % SIDE)
+    return book, spots.astype(jnp.int32)
 
 
 def pinned(x):
@@ -172,24 +205,16 @@
     cap = slots // devices
     subs = pq_codes.shape[1]
     f32 = jnp.float32
-    my_row = lax.axis_index("row")
-    core = my_row % 2
-
-    coord = lax.dynamic_index_in_dim(codebook, my_row, axis=1, keepdims=False)
-    halves = coord.reshape(2, 6, LANES)
-    piece = jnp.broadcast_to(halves[None, :, None], (row_count // 2, 2, col_count, 6, LANES))
-    piece = piece.reshape(devices, 6, LANES)
+    me = lax.axis_index("row") * col_count + lax.axis_index("col")
+
     per_row = LANES // cap
-    ids = list_ids.astype(f32).reshape(devices // per_row, 1, 1, LANES)
-    ids = jnp.broadcast_to(ids, (devices // per_row, per_row, 2, LANES)).reshape(devices, 2, LANES)
-    sent = jnp.concatenate([piece, ids], axis=1)
-    got = lax.all_to_all(sent, BOTH, 0, 0, tiled=True)
-    sibling = lax.ppermute(got, "row", [(i, i ^ 1) for i in range(row_count)])
-
-    me = my_row * col_count + lax.axis_index("col")
-    want = lax.dynamic_slice(got[:, 6], (0, (me % per_row) * cap), (devices, cap))
-    want = want.astype(jnp.int32).reshape(slots) % centroids.shape[0]
+    ids = jnp.broadcast_to(list_ids.reshape(devices // per_row, 1, 1, LANES), (devices // per_row, per_row, 1, LANES))
+    with jax.named_scope("ids"):
+        got = lax.all_to_all(ids.reshape(devices, 1, LANES), BOTH, 0, 0, tiled=True)
+    want = lax.dynamic_slice(got[:, 0], (0, (me % per_row) * cap), (devices, cap)).reshape(slots)
+    want = want % centroids.shape[0]
     start = (want // 8) * (8 * width // LANES) + want % 8
+    book, spots = gathered_book(codebook)
     vmem = pl.BlockSpec(memory_space=pltpu.VMEM)
     smem = pl.BlockSpec(memory_space=pltpu.SMEM)
     hbm = pl.BlockSpec(memory_space=pltpu.HBM)
@@ -203,12 +228,13 @@
         name="pick",
     )(start, tiled_view(centroids))
     picked = untiled_view(picked, slots, width)
-    cent = lax.all_to_all(picked.reshape(devices, cap, width), BOTH, 0, 0, tiled=True)
+    with jax.named_scope("rows"):
+        cent = lax.all_to_all(picked.reshape(devices, cap, width), BOTH, 0, 0, tiled=True)
     cent = cent.reshape(slots, width)
 
     vt, wt, a = pl.pallas_call(
         prep_kernel,
-        in_specs=[smem, vmem, vmem, vmem, vmem],
+        in_specs=[smem, vmem, vmem, vmem],
         out_specs=[vmem] * 3,
         out_shape=[
             jax.ShapeDtypeStruct((width, slots), f32),
@@ -218,11 +244,10 @@
         compiler_params=pltpu.CompilerParams(vmem_limit_bytes=24 << 20),
         name="prep",
     )(
-        core.reshape(1).astype(jnp.int32),
+        spots,
         vectors,
         pq_codes.T,
-        got.reshape(devices * 8, LANES),
-        sibling.reshape(devices * 8, LANES),
+        book,
     )
 
     slot_pos = jnp.arange(cap, dtype=jnp.int32)

time: 93.1 us -> 121 us (1.30)
  starting transfers between devices: 17 us -> 28.3 us
  local copies, waits for them, and re-layouts: 9.34 us -> 19 us
  waiting for transfers between devices: 36.4 us -> 44.7 us
    ppermute x1 -> x6, waiting for transfers between devices: 1.68 us -> 35.1 us  [moved(): return lax.ppermute(x, 'col', pairs)]
    all_to_all x1, waiting for transfers between devices: 20.9 us -> 0.01 us  [local(): lax.all_to_all(picked.reshape(devices, cap, width), BOTH, 0, 0, tiled=True)]
    ppermute x1 -> x6, starting transfers between devices: 1.29 us -> 12.2 us  [moved(): return lax.ppermute(x, 'col', pairs)]
    unnamed x20 -> x22, local copies, waits for them, and re-layouts: 8.98 us -> 15.7 us
    all_to_all x1, waiting for transfers between devices: 13.8 us -> 9.57 us  [local(): got = lax.all_to_all(ids.reshape(devices, 1, LANES), BOTH, 0, 0, tiled=True)]
    broadcast_in_dim x4 -> x1, local copies, waits for them, and re-layouts: 0.09 us -> 1.32 us  [local(): jnp.broadcast_to(list_ids.reshape(devices // per_row, 1, 1, LANES), (devi...]
  transfers between devices with their start and end apart: 3 -> 8, of which waited for: 3 -> 5; matrix products, arithmetic and copies ran while one was open for 0% -> 8% of each run, Pallas kernels for 8% -> 6%
where the time goes in v3:
time: 121 us; the launch traced here: 120 us
  waiting for transfers between devices  44.7 us (37%)
  starting transfers between devices  28.3 us (23%)
  Pallas kernels  25.7 us (21%)
  local copies, waits for them, and re-layouts  19 us (16%)
  other arithmetic  1.61 us (1%)
    ppermute x6, waiting for transfers between devices, moved(): return lax.ppermute(x, 'col', pairs)  35.1 us
    pallas_call x1, Pallas kernels, local(): pl.pallas_call(score_kernel, in_specs=[hbm, hbm, vmem, hbm, vmem], out_sp...  15.8 us
    unnamed x22, local copies, waits for them, and re-layouts  15.7 us
    ppermute x6, starting transfers between devices, moved(): return lax.ppermute(x, 'col', pairs)  12.2 us
    all_to_all x1, starting transfers between devices, local(): got = lax.all_to_all(ids.reshape(devices, 1, LANES), BOTH, 0, 0, tiled=True)  11.5 us
    all_to_all x1, waiting for transfers between devices, local(): got = lax.all_to_all(ids.reshape(devices, 1, LANES), BOTH, 0, 0, tiled=True)  9.57 us
    pallas_call x1, Pallas kernels, local(): pl.pallas_call(prep_kernel, in_specs=[smem, vmem, vmem, vmem], out_specs=...  6.83 us
    all_to_all x1, starting transfers between devices, local(): lax.all_to_all(picked.reshape(devices, cap, width), BOTH, 0, 0, tiled=True)  4.6 us
  transfers between devices with their start and end apart: 8, of which 5 were waited for; matrix products, arithmetic and copies ran while one was open for 8% of the time, Pallas kernels for 6%

profile of v3, /device:TPU:1, one launch (start us, length us, event | category | flops | bytes accessed | tf_op | source)
XLA Modules:
  0.0 120.2 jit_solution(15780482228987682145)
XLA Ops:
  0.6 1.3 %broadcast_in_dim.16 = s32[8,16,128]{2,1,0:T(8,128)} broadcast(s32[8,128]{1,0:T(8,128)} %bitcast.26), dimensions={0,2} | broadcast | bytes 69632 | tf_op jit(solution)/shard_map/broadcast_in_dim | solution.py:211
  2.0 11.5 %all-to-all-start = ((s32[128,1,128]{2,1,0:T(1,128)}), s32[128,1,128]{2,1,0:T(1,128)S(1)}, u32[]{:S(2)}, u32[]{:S(2)}) async-start(s32[128,1,128]{2,1,0:T(1,128)} %bitcast.3), calls=%async_computation | async-start | bytes 131072 | tf_op jit(solution)/shard_map/ids/all_to_all | solution.py:213
  13.5 9.6 %all-to-all-done = s32[128,1,128]{2,1,0:T(1,128)S(1)} async-done(((s32[128,1,128]{2,1,0:T(1,128)}), s32[128,1,128]{2,1,0:T(1,128)S(1)}, u32[]{:S(2)}, u32[]{:S(2)}) %all-to-all-start) | async-done | bytes 65568 | tf_op jit(solution)/shard_map/ids/all_to_all | solution.py:213
  23.4 1.4 %copy-done.4 = f32[512,768]{1,0:T(8,128)S(1)} copy-done((f32[512,768]{1,0:T(8,128)S(1)}, f32[512,768]{1,0:T(8,128)}, u32[]{:S(2)}) %copy-start.4) | copy-done | bytes 1572888
  24.8 3.0 %pick.1 = f32[6144,128]{1,0:T(8,128)} custom-call(s32[1024]{0:T(1024)S(1)} %fusion.3.start_ref, f32[3072,128]{1,0:T(8,128)S(1)} %bitcast.20), custom_call_target="tpu_custom_call" | custom-call | tf_op jit(solution)/shard_map/pick/pallas_call | solution.py:221
  27.9 4.6 %all-to-all-start.1 = ((f32[128,8,768]{2,1,0:T(8,128)}), f32[128,8,768]{2,1,0:T(8,128)S(1)}, u32[]{:S(2)}, u32[]{:S(2)}) async-start(f32[128,8,768]{2,1,0:T(8,128)} %bitcast.22), calls=%async_computation.1 | async-start | bytes 6291456 | tf_op jit(solution)/shard_map/rows/all_to_all | solution.py:232
  32.5 3.4 %collective-permute-start.1 = (f32[48,256]{1,0:T(8,128)}, f32[48,256]{1,0:T(8,128)}, u32[]{:S(2)}, u32[]{:S(2)}) collective-permute-start(f32[48,256]{1,0:T(8,128)} %bitcast.23), channel_id=1, source_target_pairs={{0,3},{1,0},{2,1},{3,2},{4,7},{5,4},{6,5},{7,6},{8,11},{9,8},{10,9... | collective-permute-start | bytes 147464 | tf_op jit(solution)/shard_map/book1/ppermute | solution.py:170
  36.6 1.4 %constant_dynamic-update-slice_fusion.6 = f32[768,256]{1,0:T(8,128)} fusion(f32[6,8,256]{2,1,0:T(8,128)} %param.11), kind=kLoop, calls=%fused_computation.10 | loop fusion | bytes 98304
  38.1 0.9 reshape.75.live_ref
  39.0 20.8 %collective-permute-done = f32[48,256]{1,0:T(8,128)} collective-permute-done((f32[48,256]{1,0:T(8,128)}, f32[48,256]{1,0:T(8,128)}, u32[]{:S(2)}, u32[]{:S(2)}) %collective-permute-start) | collective-permute-done | bytes 49184 | tf_op jit(solution)/shard_map/book1/ppermute | solution.py:170
  59.8 1.4 %constant_dynamic-update-slice_fusion.5 = f32[768,256]{1,0:T(8,128)} fusion(f32[768,256]{1,0:T(8,128)} %constant_dynamic-update-slice_fusion.6, f32[48,256]{1,0:T(8,128)} %collective-permute-done), kind=kLoop, calls=%fused_computation.9 | loop fusion | bytes 98304
  61.3 6.1 %collective-permute-done.2 = f32[48,256]{1,0:T(8,128)S(1)} collective-permute-done((f32[48,256]{1,0:T(8,128)}, f32[48,256]{1,0:T(8,128)S(1)}, u32[]{:S(2)}, u32[]{:S(2)}) %collective-permute-start.2) | collective-permute-done | bytes 49184 | tf_op jit(solution)/shard_map/book2/ppermute | solution.py:170
  68.3 7.0 %collective-permute-start.3 = (f32[192,256]{1,0:T(8,128)S(1)}, f32[192,256]{1,0:T(8,128)S(1)}, u32[]{:S(2)}, u32[]{:S(2)}) collective-permute-start(f32[192,256]{1,0:T(8,128)S(1)} %pad_maximum_fusion), channel_id=1, source_target_pairs={{0,4},{1,5},{2,6},{3,7},{4,8},{5,9},{6,10},{7,11},{8,12},{9,13},{1... | collective-permute-start | bytes 589832 | tf_op jit(solution)/shard_map/book3/ppermute | solution.py:170
  75.3 1.4 %constant_dynamic-update-slice_fusion.4 = f32[768,256]{1,0:T(8,128)} fusion(f32[768,256]{1,0:T(8,128)} %constant_dynamic-update-slice_fusion.5, f32[48,256]{1,0:T(8,128)} %collective-permute-done.1), kind=kLoop, calls=%fused_computation.8 | loop fusion | bytes 98304
  76.7 1.7 %collective-permute-start.4 = (f32[192,256]{1,0:T(8,128)S(1)}, f32[192,256]{1,0:T(8,128)S(1)}, u32[]{:S(2)}, u32[]{:S(2)}) collective-permute-start(f32[192,256]{1,0:T(8,128)S(1)} %pad_maximum_fusion), channel_id=1, source_target_pairs={{0,12},{1,13},{2,14},{3,15},{4,0},{5,1},{6,2},{7,3},{8,4},{9,5},{1... | collective-permute-start | bytes 589832 | tf_op jit(solution)/shard_map/book3/ppermute | solution.py:170
  79.0 2.8 %collective-permute-done.3 = f32[192,256]{1,0:T(8,128)S(1)} collective-permute-done((f32[192,256]{1,0:T(8,128)S(1)}, f32[192,256]{1,0:T(8,128)S(1)}, u32[]{:S(2)}, u32[]{:S(2)}) %collective-permute-start.3) | collective-permute-done | bytes 196640 | tf_op jit(solution)/shard_map/book3/ppermute | solution.py:170
  83.2 5.3 %collective-permute-done.5 = f32[192,256]{1,0:T(8,128)S(1)} collective-permute-done((f32[192,256]{1,0:T(8,128)S(1)}, f32[192,256]{1,0:T(8,128)S(1)}, u32[]{:S(2)}, u32[]{:S(2)}) %collective-permute-start.5) | collective-permute-done | bytes 196640 | tf_op jit(solution)/shard_map/book4/ppermute | solution.py:170
  89.3 1.9 %copy-done = f32[1024,768]{1,0:T(8,128)S(1)} copy-done((f32[1024,768]{1,0:T(8,128)S(1)}, f32[1024,768]{1,0:T(8,128)}, u32[]{:S(2)}) %copy-start) | copy-done | bytes 3145752
  91.2 1.1 copy-done.5
  92.3 6.8 %prep.1 = (f32[768,1024]{1,0:T(8,128)S(1)}, f32[768,1024]{1,0:T(8,128)S(1)}, bf16[48,256,128]{2,1,0:T(8,128)(2,1)S(1)}) custom-call(s32[16]{0:T(128)S(1)} %fusion.11.spot_ref, f32[1024,768]{1,0:T(8,128)S(1)} %copy-done, s32[96,1024]{1,0:T(8,128)S(1)} %bitcast.21, f32[768,256]{1,0:T(8,128)S(1)} %copy-done.5), custom_call_target="tpu_custom_call" | custom-call | tf_op jit(solution)/shard_map/prep/pallas_call | solution.py:235
  99.1 1.7 %copy-done.1 = f32[768,1024]{1,0:T(8,128)} copy-done((f32[768,1024]{1,0:T(8,128)}, f32[768,1024]{1,0:T(8,128)S(1)}, u32[]{:S(2)}) %copy-start.1) | copy-done | bytes 3145752
  100.8 1.7 %copy-done.2 = f32[768,1024]{1,0:T(8,128)} copy-done((f32[768,1024]{1,0:T(8,128)}, f32[768,1024]{1,0:T(8,128)S(1)}, u32[]{:S(2)}) %copy-start.2) | copy-done | bytes 3145752
  102.5 1.7 %copy-done.3 = bf16[48,256,128]{2,1,0:T(8,128)(2,1)} copy-done((bf16[48,256,128]{2,1,0:T(8,128)(2,1)}, bf16[48,256,128]{2,1,0:T(8,128)(2,1)S(1)}, u32[]{:S(2)}) %copy-start.3) | copy-done | bytes 3145752
  104.2 15.8 %score.1 = (f32[1,1024]{1,0:T(1,128)}, f32[1,1024]{1,0:T(1,128)}) custom-call(f32[768,1024]{1,0:T(8,128)} %copy-done.1, f32[768,1024]{1,0:T(8,128)} %copy-done.2, f32[1024,768]{1,0:T(8,128)S(1)} %bitcast.19, bf16[48,256,128]{2,1,0:T(8,128)(2,1)} %copy-done.3, s32[1,1024]{1,0:T(1,128)S(1)} %reshape.75.live_ref), custom_call_target="tpu_custom_call" | custom-call | tf_op jit(solution)/shard_map/score/pallas_call | solution.py:255
  (26 shorter events, 4.6 us)
Async XLA Ops:
  2.0 21.1 %all-to-all-start = ((s32[128,1,128]{2,1,0:T(1,128)}), s32[128,1,128]{2,1,0:T(1,128)S(1)}, u32[]{:S(2)}, u32[]{:S(2)}) async-start(s32[128,1,128]{2,1,0:T(1,128)} %bitcast.3), calls=%async_computation | async-start | bytes 131072 | tf_op jit(solution)/shard_map/ids/all_to_all | solution.py:213
  23.4 1.4 %copy-start.4 = (f32[512,768]{1,0:T(8,128)S(1)}, f32[512,768]{1,0:T(8,128)}, u32[]{:S(2)}) copy-start(f32[512,768]{1,0:T(8,128)} %param.10) | copy-start | bytes 4718596
  27.8 8.1 %copy-start.7 = (s32[1,128]{1,0:T(1,128)S(1)}, s32[1,128]{1,0:T(1,128)}, u32[]{:S(2)}) copy-start(s32[1,128]{1,0:T(1,128)} %param.9) | copy-start | bytes 1540
  27.9 61.4 %copy-start.6 = (s32[1024,96]{0,1:T(8,128)S(1)}, s32[1024,96]{0,1:T(8,128)}, u32[]{:S(2)}) copy-start(s32[1024,96]{0,1:T(8,128)} %param.8) | copy-start | bytes 1179652
  27.9 76.3 %all-to-all-start.1 = ((f32[128,8,768]{2,1,0:T(8,128)}), f32[128,8,768]{2,1,0:T(8,128)S(1)}, u32[]{:S(2)}, u32[]{:S(2)}) async-start(f32[128,8,768]{2,1,0:T(8,128)} %bitcast.22), calls=%async_computation.1 | async-start | bytes 6291456 | tf_op jit(solution)/shard_map/rows/all_to_all | solution.py:232
  32.5 28.8 %collective-permute-start.1 = (f32[48,256]{1,0:T(8,128)}, f32[48,256]{1,0:T(8,128)}, u32[]{:S(2)}, u32[]{:S(2)}) collective-permute-start(f32[48,256]{1,0:T(8,128)} %bitcast.23), channel_id=1, source_target_pairs={{0,3},{1,0},{2,1},{3,2},{4,7},{5,4},{6,5},{7,6},{8,11},{9,8},{10,9... | collective-permute-start | bytes 147464 | tf_op jit(solution)/shard_map/book1/ppermute | solution.py:170
  35.9 23.9 %collective-permute-start = (f32[48,256]{1,0:T(8,128)}, f32[48,256]{1,0:T(8,128)}, u32[]{:S(2)}, u32[]{:S(2)}) collective-permute-start(f32[48,256]{1,0:T(8,128)} %bitcast.24), channel_id=1, source_target_pairs={{0,1},{1,2},{2,3},{3,0},{4,5},{5,6},{6,7},{7,4},{8,9},{9,10},{10,1... | collective-permute-start | bytes 147464 | tf_op jit(solution)/shard_map/book1/ppermute | solution.py:170
  59.8 7.6 %collective-permute-start.2 = (f32[48,256]{1,0:T(8,128)}, f32[48,256]{1,0:T(8,128)S(1)}, u32[]{:S(2)}, u32[]{:S(2)}) collective-permute-start(f32[48,256]{1,0:T(8,128)} %collective-permute-done), channel_id=1, source_target_pairs={{0,1},{1,2},{2,3},{3,0},{4,5},{5,6},{6,7},{7,4},{8,9},{9,10},{10,1... | collective-permute-start | bytes 147464 | tf_op jit(solution)/shard_map/book2/ppermute | solution.py:170
  68.3 13.6 %collective-permute-start.3 = (f32[192,256]{1,0:T(8,128)S(1)}, f32[192,256]{1,0:T(8,128)S(1)}, u32[]{:S(2)}, u32[]{:S(2)}) collective-permute-start(f32[192,256]{1,0:T(8,128)S(1)} %pad_maximum_fusion), channel_id=1, source_target_pairs={{0,4},{1,5},{2,6},{3,7},{4,8},{5,9},{6,10},{7,11},{8,12},{9,13},{1... | collective-permute-start | bytes 589832 | tf_op jit(solution)/shard_map/book3/ppermute | solution.py:170
  76.7 5.8 %collective-permute-start.4 = (f32[192,256]{1,0:T(8,128)S(1)}, f32[192,256]{1,0:T(8,128)S(1)}, u32[]{:S(2)}, u32[]{:S(2)}) collective-permute-start(f32[192,256]{1,0:T(8,128)S(1)} %pad_maximum_fusion), channel_id=1, source_target_pairs={{0,12},{1,13},{2,14},{3,15},{4,0},{5,1},{6,2},{7,3},{8,4},{9,5},{1... | collective-permute-start | bytes 589832 | tf_op jit(solution)/shard_map/book3/ppermute | solution.py:170
  81.9 6.7 %collective-permute-start.5 = (f32[192,256]{1,0:T(8,128)S(1)}, f32[192,256]{1,0:T(8,128)S(1)}, u32[]{:S(2)}, u32[]{:S(2)}) collective-permute-start(f32[192,256]{1,0:T(8,128)S(1)} %collective-permute-done.3), channel_id=1, source_target_pairs={{0,4},{1,5},{2,6},{3,7},{4,8},{5,9},{6,10},{7,11},{8,12},{9,13},{1... | collective-permute-start | bytes 589832 | tf_op jit(solution)/shard_map/book4/ppermute | solution.py:170
  89.3 1.9 %copy-start = (f32[1024,768]{1,0:T(8,128)S(1)}, f32[1024,768]{1,0:T(8,128)}, u32[]{:S(2)}) copy-start(f32[1024,768]{1,0:T(8,128)} %vec_ref.1) | copy-start | bytes 9437188
  91.2 1.1 copy-start.5
  99.1 1.7 %copy-start.1 = (f32[768,1024]{1,0:T(8,128)}, f32[768,1024]{1,0:T(8,128)S(1)}, u32[]{:S(2)}) copy-start(f32[768,1024]{1,0:T(8,128)S(1)} %get-tuple-element.7.vt_hbm) | copy-start | bytes 9437188
  100.8 1.7 %copy-start.2 = (f32[768,1024]{1,0:T(8,128)}, f32[768,1024]{1,0:T(8,128)S(1)}, u32[]{:S(2)}) copy-start(f32[768,1024]{1,0:T(8,128)S(1)} %get-tuple-element.8.wt_hbm) | copy-start | bytes 9437188
  102.5 1.7 %copy-start.3 = (bf16[48,256,128]{2,1,0:T(8,128)(2,1)}, bf16[48,256,128]{2,1,0:T(8,128)(2,1)S(1)}, u32[]{:S(2)}) copy-start(bf16[48,256,128]{2,1,0:T(8,128)(2,1)S(1)} %get-tuple-element.9.a_hbm) | copy-start | bytes 9437188

commit v4 on v3

--- a/solution.py
+++ b/solution.py
@@ -18,7 +18,8 @@
     return hi, mid, lo
 
 
-def prep_kernel(spot_ref, vec_ref, codes_ref, book_ref, vt_ref, wt_ref, a_ref):
+def prep_kernel(core_ref, vec_ref, codes_ref, own_ref, sib_ref, vt_ref, wt_ref, a_ref):
+    core = core_ref[0]
     rows, width = vec_ref.shape
     sublane = lax.broadcasted_iota(jnp.int32, (8, 256), 0)
     for block in range(width // LANES):
@@ -32,9 +33,14 @@
         stack = []
         for i in range(8):
             m = step * 8 + i
-            at = pl.multiple_of((spot_ref[m // 6] * 6 + m % 6) * 8, 8)
-            both = book_ref[pl.ds(at, 8), :]
-            words = [both[:, :LANES], both[:, LANES:]]
+            shard, within = m // 6, m % 6
+            half, j = within // 3, within % 3
+            base = shard * 8 + j * 2
+            mine = half == core
+            words = []
+            for h in range(2):
+                spot = pl.ds(base + h, 8, stride=LANES)
+                words.append(jnp.where(mine, own_ref[spot, :], sib_ref[spot, :]))
             at = pl.ds(pl.multiple_of(m * 8, 8), 8)
             for g in range(rows // LANES):
                 cut = slice(g * LANES, (g + 1) * LANES)
@@ -43,6 +49,7 @@
                 first = jnp.take_along_axis(words[0], low, axis=1, mode="promise_in_bounds")
                 second = jnp.take_along_axis(words[1], low, axis=1, mode="promise_in_bounds")
                 wt_ref[at, cut] = vt_ref[at, cut] - jnp.where(code >= LANES, second, first)
+            both = jnp.concatenate(words, axis=1)
             norm = jnp.sum(both * both, axis=0, keepdims=True)
             hi, mid, lo = three_way(-2.0 * both)
             nhi, nmid, nlo = three_way(norm)
@@ -159,38 +166,29 @@
     best_ref[...] = jnp.where(live, best, 0.0)
 
 
-SIDE = 4
-
-
-def moved(x, dy, dz):
-    pairs = []
-    for y in range(SIDE):
-        for z in range(SIDE):
-            pairs.append((y * SIDE + z, (y + dy) % SIDE * SIDE + (z + dz) % SIDE))
-    return lax.ppermute(x, "col", pairs)
-
-
-def gathered_book(codebook):
-    mine = codebook.reshape(-1, codebook.shape[2])
-    with jax.named_scope("book1"):
-        back, ahead = moved(mine, 0, 1), moved(mine, 0, -1)
-    with jax.named_scope("book2"):
-        far = moved(back, 0, 1)
-    line = jnp.concatenate([mine, back, ahead, far])
-    with jax.named_scope("book3"):
-        back, ahead = moved(line, 1, 0), moved(line, -1, 0)
-    with jax.named_scope("book4"):
-        far = moved(back, 1, 0)
-    book = jnp.concatenate([line, back, ahead, far])
-    col = lax.axis_index("col")
-    shard = jnp.arange(SIDE * SIDE, dtype=jnp.int32)
-
-    def place(theirs, own):
-        ahead_by = (theirs - own) % SIDE
-        return jnp.where(ahead_by == SIDE - 1, 1, jnp.where(ahead_by == 0, 0, ahead_by + 1))
-
-    spots = place(shard // SIDE, col // SIDE) * SIDE + place(shard % SIDE, col % SIDE)
-    return book, spots.astype(jnp.int32)
+def pack_kernel(ids_hbm, book_hbm, lists_hbm, out_hbm, lists_ref, ids_ref, book_ref, out_ref, sems):
+    fetches = [
+        pltpu.make_async_copy(book_hbm, book_ref, sems.at[0]),
+        pltpu.make_async_copy(ids_hbm, ids_ref, sems.at[1]),
+        pltpu.make_async_copy(lists_hbm, lists_ref, sems.at[2]),
+    ]
+    for fetch in fetches:
+        fetch.start()
+    u = lax.axis_index("row")
+    rows = ids_ref.shape[0]
+    cols = out_ref.shape[0] // rows
+    fetches[0].wait()
+    fetches[1].wait()
+    mine = book_ref[pl.ds(u, 12, stride=8), :]
+    for r in range(rows):
+        half = mine[(r % 2) * 6 : (r % 2) * 6 + 6, :]
+        ids = ids_ref[r : r + 1, :].astype(jnp.float32)
+        tile = jnp.concatenate([half, ids, ids], axis=0)
+        out_ref[r * cols : (r + 1) * cols] = jnp.broadcast_to(tile[None], (cols, 8, LANES))
+    send = pltpu.make_async_copy(out_ref, out_hbm, sems.at[3])
+    send.start()
+    fetches[2].wait()
+    send.wait()
 
 
 def pinned(x):
@@ -205,19 +203,41 @@
     cap = slots // devices
     subs = pq_codes.shape[1]
     f32 = jnp.float32
-    me = lax.axis_index("row") * col_count + lax.axis_index("col")
+    my_row = lax.axis_index("row")
+    core = my_row % 2
 
     per_row = LANES // cap
-    ids = jnp.broadcast_to(list_ids.reshape(devices // per_row, 1, 1, LANES), (devices // per_row, per_row, 1, LANES))
-    with jax.named_scope("ids"):
-        got = lax.all_to_all(ids.reshape(devices, 1, LANES), BOTH, 0, 0, tiled=True)
-    want = lax.dynamic_slice(got[:, 0], (0, (me % per_row) * cap), (devices, cap)).reshape(slots)
-    want = want % centroids.shape[0]
-    start = (want // 8) * (8 * width // LANES) + want % 8
-    book, spots = gathered_book(codebook)
     vmem = pl.BlockSpec(memory_space=pltpu.VMEM)
     smem = pl.BlockSpec(memory_space=pltpu.SMEM)
     hbm = pl.BlockSpec(memory_space=pltpu.HBM)
+    sent, lists = pl.pallas_call(
+        pack_kernel,
+        in_specs=[hbm, hbm, hbm],
+        out_specs=[hbm, vmem],
+        out_shape=[
+            pltpu.HBM((devices, 8, LANES), f32),
+            pltpu.VMEM((centroids.size // LANES, LANES), f32),
+        ],
+        scratch_shapes=[
+            pltpu.VMEM((row_count, LANES), jnp.int32),
+            pltpu.VMEM((codebook.size // LANES, LANES), f32),
+            pltpu.VMEM((devices, 8, LANES), f32),
+            pltpu.SemaphoreType.DMA((4,)),
+        ],
+        compiler_params=pltpu.CompilerParams(vmem_limit_bytes=4 << 20),
+        name="pack",
+    )(
+        pinned(list_ids.reshape(row_count, LANES)),
+        pinned(tiled_view(codebook.reshape(-1, codebook.shape[2]))),
+        pinned(tiled_view(centroids)),
+    )
+    got = lax.all_to_all(sent, BOTH, 0, 0, tiled=True)
+    sibling = lax.ppermute(got, "row", [(i, i ^ 1) for i in range(row_count)])
+
+    me = my_row * col_count + lax.axis_index("col")
+    want = lax.dynamic_slice(got[:, 6], (0, (me % per_row) * cap), (devices, cap))
+    want = want.astype(jnp.int32).reshape(slots) % centroids.shape[0]
+    start = (want // 8) * (8 * width // LANES) + want % 8
     picked = pl.pallas_call(
         pick_kernel,
         in_specs=[smem, vmem],
@@ -226,15 +246,14 @@
         scratch_shapes=[pltpu.VMEM((slots * width // LANES, LANES), f32), pltpu.SemaphoreType.DMA((PARTS,))],
         compiler_params=pltpu.CompilerParams(vmem_limit_bytes=8 << 20),
         name="pick",
-    )(start, tiled_view(centroids))
+    )(start, lists)
     picked = untiled_view(picked, slots, width)
-    with jax.named_scope("rows"):
-        cent = lax.all_to_all(picked.reshape(devices, cap, width), BOTH, 0, 0, tiled=True)
+    cent = lax.all_to_all(picked.reshape(devices, cap, width), BOTH, 0, 0, tiled=True)
     cent = cent.reshape(slots, width)
 
     vt, wt, a = pl.pallas_call(
         prep_kernel,
-        in_specs=[smem, vmem, vmem, vmem],
+        in_specs=[smem, vmem, vmem, vmem, vmem],
         out_specs=[vmem] * 3,
         out_shape=[
             jax.ShapeDtypeStruct((width, slots), f32),
@@ -244,10 +263,11 @@
         compiler_params=pltpu.CompilerParams(vmem_limit_bytes=24 << 20),
         name="prep",
     )(
-        spots,
+        core.reshape(1).astype(jnp.int32),
         vectors,
         pq_codes.T,
-        book,
+        got.reshape(devices * 8, LANES),
+        sibling.reshape(devices * 8, LANES),
     )
 
     slot_pos = jnp.arange(cap, dtype=jnp.int32)

time: 121 us -> 92.9 us (0.77)
  starting transfers between devices: 28.3 us -> 17.2 us
  local copies, waits for them, and re-layouts: 19 us -> 9.07 us
  waiting for transfers between devices: 44.7 us -> 36 us
  Pallas kernels: 25.7 us -> 28.3 us
    ppermute x6 -> x1, waiting for transfers between devices: 35.1 us -> 0.24 us  [local(): sibling = lax.ppermute(got, 'row', [(i, i ^ 1) for i in range(row_count)])]
    all_to_all x1, waiting for transfers between devices: 0.01 us -> 21.9 us  [local(): lax.all_to_all(picked.reshape(devices, cap, width), BOTH, 0, 0, tiled=True)]
    ppermute x6 -> x1, starting transfers between devices: 12.2 us -> 1.29 us  [local(): sibling = lax.ppermute(got, 'row', [(i, i ^ 1) for i in range(row_count)])]
    unnamed x22 -> x16, local copies, waits for them, and re-layouts: 15.7 us -> 7.98 us
    all_to_all x1, waiting for transfers between devices: 9.57 us -> 13.8 us  [local(): got = lax.all_to_all(sent, BOTH, 0, 0, tiled=True)]
    pallas_call x1 -> x2, Pallas kernels: 6.83 us -> 9.47 us  [the longest x1 7.8 us: local(): pl.pallas_call(prep_kernel, in_specs=[smem, vmem, vmem, vmem, vmem], out_...]
    broadcast_in_dim x1 -> x0, local copies, waits for them, and re-layouts: 1.32 us -> none  [local(): jnp.broadcast_to(list_ids.reshape(devices // per_row, 1, 1, LANES), (devi...]
  transfers between devices with their start and end apart: 8 -> 3, of which waited for: 5 -> 3; matrix products, arithmetic and copies ran while one was open for 8% -> 2% of each run, Pallas kernels for 6% -> 8%
where the time goes in v4:
time: 92.9 us; the launch traced here: 92.5 us
  waiting for transfers between devices  36 us (39%)
  Pallas kernels  28.3 us (30%)
  starting transfers between devices  17.2 us (19%)
  local copies, waits for them, and re-layouts  9.07 us (10%)
  other arithmetic  0.98 us (1%)
    all_to_all x1, waiting for transfers between devices, local(): lax.all_to_all(picked.reshape(devices, cap, width), BOTH, 0, 0, tiled=True)  21.9 us
    pallas_call x1, Pallas kernels, local(): pl.pallas_call(score_kernel, in_specs=[hbm, hbm, vmem, hbm, vmem], out_sp...  15.8 us
    all_to_all x1, waiting for transfers between devices, local(): got = lax.all_to_all(sent, BOTH, 0, 0, tiled=True)  13.8 us
    all_to_all x1, starting transfers between devices, local(): got = lax.all_to_all(sent, BOTH, 0, 0, tiled=True)  11.5 us
    unnamed x16, local copies, waits for them, and re-layouts  7.98 us
    pallas_call x1, Pallas kernels, local(): pl.pallas_call(prep_kernel, in_specs=[smem, vmem, vmem, vmem, vmem], out_...  7.8 us
    all_to_all x1, starting transfers between devices, local(): lax.all_to_all(picked.reshape(devices, cap, width), BOTH, 0, 0, tiled=True)  4.41 us
    pallas_call x1, Pallas kernels, local(): pl.pallas_call(pick_kernel, in_specs=[smem, vmem], out_specs=hbm, out_sha...  3.03 us
  transfers between devices with their start and end apart: 3, of which 3 were waited for; matrix products, arithmetic and copies ran while one was open for 2% of the time, Pallas kernels for 8%

profile of v4, /device:TPU:1, one launch (start us, length us, event | category | flops | bytes accessed | tf_op | source)
XLA Modules:
  0.0 92.5 jit_solution(18429908644995094440)
XLA Ops:
  0.6 1.7 %pack.1 = (f32[128,8,128]{2,1,0:T(8,128)}, f32[3072,128]{1,0:T(8,128)S(1)}) custom-call(s32[8,128]{1,0:T(8,128)} %bitcast.30, f32[96,128]{1,0:T(8,128)} %bitcast.29, f32[3072,128]{1,0:T(8,128)} %bitcast.28), custom_call_target="tpu_custom_call" | custom-call | tf_op jit(solution)/shard_map/pack/pallas_call | solution.py:213
  2.3 11.5 %all-to-all-start = ((f32[128,8,128]{2,1,0:T(8,128)}), f32[128,8,128]{2,1,0:T(8,128)S(1)}, u32[]{:S(2)}, u32[]{:S(2)}) async-start(f32[128,8,128]{2,1,0:T(8,128)} %get-tuple-element.9), calls=%async_computation | async-start | bytes 1048576 | tf_op jit(solution)/shard_map/all_to_all | solution.py:234
  13.8 13.8 %all-to-all-done = f32[128,8,128]{2,1,0:T(8,128)S(1)} async-done(((f32[128,8,128]{2,1,0:T(8,128)}), f32[128,8,128]{2,1,0:T(8,128)S(1)}, u32[]{:S(2)}, u32[]{:S(2)}) %all-to-all-start) | async-done | bytes 524320 | tf_op jit(solution)/shard_map/all_to_all | solution.py:234
  27.7 0.1 slice.4
  27.7 0.3 convert_reduce_fusion
  28.0 0.1 convert_element_type.21
  28.1 3.0 %pick.1 = f32[6144,128]{1,0:T(8,128)} custom-call(s32[1024]{0:T(1024)S(1)} %fusion.3.start_ref, f32[3072,128]{1,0:T(8,128)S(1)} %get-tuple-element.12.cent_ref), custom_call_target="tpu_custom_call" | custom-call | tf_op jit(solution)/shard_map/pick/pallas_call | solution.py:241
  31.1 0.0 copy-start.7
  31.2 0.0 copy-start.6
  31.2 0.0 copy-done.4
  31.2 4.4 %all-to-all-start.1 = ((f32[128,8,768]{2,1,0:T(8,128)}), f32[128,8,768]{2,1,0:T(8,128)S(1)}, u32[]{:S(2)}, u32[]{:S(2)}) async-start(f32[128,8,768]{2,1,0:T(8,128)} %bitcast.27), calls=%async_computation.1 | async-start | bytes 6291456 | tf_op jit(solution)/shard_map/all_to_all | solution.py:251
  35.6 1.3 %collective-permute-start = (f32[128,8,128]{2,1,0:T(8,128)}, f32[128,8,128]{2,1,0:T(8,128)}, u32[]{:S(2)}, u32[]{:S(2)}) collective-permute-start(f32[128,8,128]{2,1,0:T(8,128)} %copy-done.4), channel_id=1, source_target_pairs={{0,16},{16,0},{32,48},{48,32},{64,80},{80,64},{96,112},{112,96},{1... | collective-permute-start | bytes 1572872 | tf_op jit(solution)/shard_map/ppermute | solution.py:235
  36.9 0.0 copy-done.7
  36.9 0.7 fusion
  37.6 0.9 %reshape.81.live_ref = s32[1,1024]{1,0:T(1,128)S(1)} reshape(s32[128,8]{1,0:T(8,128)} %fusion) | data formatting | bytes 8192 | tf_op jit(solution)/shard_map/convert_element_type | solution.py:274
  38.5 0.2 collective-permute-done
  38.8 1.9 %copy-done = f32[1024,768]{1,0:T(8,128)S(1)} copy-done((f32[1024,768]{1,0:T(8,128)S(1)}, f32[1024,768]{1,0:T(8,128)}, u32[]{:S(2)}) %copy-start) | copy-done | bytes 3145752
  40.7 1.0 %copy-done.5 = f32[128,8,128]{2,1,0:T(8,128)S(1)} copy-done((f32[128,8,128]{2,1,0:T(8,128)S(1)}, f32[128,8,128]{2,1,0:T(8,128)}, u32[]{:S(2)}) %copy-start.5) | copy-done | bytes 524312
  41.7 7.8 %prep.1 = (f32[768,1024]{1,0:T(8,128)S(1)}, f32[768,1024]{1,0:T(8,128)S(1)}, bf16[48,256,128]{2,1,0:T(8,128)(2,1)S(1)}) custom-call(s32[1]{0:T(128)} %bitcast.core_ref, f32[1024,768]{1,0:T(8,128)S(1)} %copy-done, s32[96,1024]{1,0:T(8,128)S(1)} %bitcast.26, f32[1024,128]{1,0:T(8,128)S(1)} %bitcast.25, f32[1024,128]{1,0:T(8,128)} %bitcast.10.sib_ref), custom_call_target="tpu_custom_call" | custom-call | tf_op jit(solution)/shard_map/prep/pallas_call | solution.py:254
  49.5 1.7 %copy-done.1 = f32[768,1024]{1,0:T(8,128)} copy-done((f32[768,1024]{1,0:T(8,128)}, f32[768,1024]{1,0:T(8,128)S(1)}, u32[]{:S(2)}) %copy-start.1) | copy-done | bytes 3145752
  51.2 1.7 %copy-done.2 = f32[768,1024]{1,0:T(8,128)} copy-done((f32[768,1024]{1,0:T(8,128)}, f32[768,1024]{1,0:T(8,128)S(1)}, u32[]{:S(2)}) %copy-start.2) | copy-done | bytes 3145752
  52.9 1.7 %copy-done.3 = bf16[48,256,128]{2,1,0:T(8,128)(2,1)} copy-done((bf16[48,256,128]{2,1,0:T(8,128)(2,1)}, bf16[48,256,128]{2,1,0:T(8,128)(2,1)S(1)}, u32[]{:S(2)}) %copy-start.3) | copy-done | bytes 3145752
  54.6 21.9 %all-to-all-done.1 = f32[128,8,768]{2,1,0:T(8,128)S(1)} async-done(((f32[128,8,768]{2,1,0:T(8,128)}), f32[128,8,768]{2,1,0:T(8,128)S(1)}, u32[]{:S(2)}, u32[]{:S(2)}) %all-to-all-start.1) | async-done | bytes 3145760 | tf_op jit(solution)/shard_map/all_to_all | solution.py:251
  76.4 15.8 %score.1 = (f32[1,1024]{1,0:T(1,128)}, f32[1,1024]{1,0:T(1,128)}) custom-call(f32[768,1024]{1,0:T(8,128)} %copy-done.1, f32[768,1024]{1,0:T(8,128)} %copy-done.2, f32[1024,768]{1,0:T(8,128)S(1)} %bitcast.24, bf16[48,256,128]{2,1,0:T(8,128)(2,1)} %copy-done.3, s32[1,1024]{1,0:T(1,128)S(1)} %reshape.81.live_ref), custom_call_target="tpu_custom_call" | custom-call | tf_op jit(solution)/shard_map/score/pallas_call | solution.py:275
  (8 shorter events, 0.0 us)
Async XLA Ops:
  2.3 25.4 %all-to-all-start = ((f32[128,8,128]{2,1,0:T(8,128)}), f32[128,8,128]{2,1,0:T(8,128)S(1)}, u32[]{:S(2)}, u32[]{:S(2)}) async-start(f32[128,8,128]{2,1,0:T(8,128)} %get-tuple-element.9), calls=%async_computation | async-start | bytes 1048576 | tf_op jit(solution)/shard_map/all_to_all | solution.py:234
  27.7 3.5 %copy-start.4 = (f32[128,8,128]{2,1,0:T(8,128)}, f32[128,8,128]{2,1,0:T(8,128)S(1)}, u32[]{:S(2)}) copy-start(f32[128,8,128]{2,1,0:T(8,128)S(1)} %all-to-all-done) | copy-start | bytes 1572868
  31.1 5.7 %copy-start.7 = (s32[1,128]{1,0:T(1,128)S(1)}, s32[1,128]{1,0:T(1,128)}, u32[]{:S(2)}) copy-start(s32[1,128]{1,0:T(1,128)} %param.9) | copy-start | bytes 1540
  31.2 7.6 %copy-start.6 = (s32[1024,96]{0,1:T(8,128)S(1)}, s32[1024,96]{0,1:T(8,128)}, u32[]{:S(2)}) copy-start(s32[1024,96]{0,1:T(8,128)} %param.8) | copy-start | bytes 1179652
  31.2 45.3 %all-to-all-start.1 = ((f32[128,8,768]{2,1,0:T(8,128)}), f32[128,8,768]{2,1,0:T(8,128)S(1)}, u32[]{:S(2)}, u32[]{:S(2)}) async-start(f32[128,8,768]{2,1,0:T(8,128)} %bitcast.27), calls=%async_computation.1 | async-start | bytes 6291456 | tf_op jit(solution)/shard_map/all_to_all | solution.py:251
  35.6 3.2 %collective-permute-start = (f32[128,8,128]{2,1,0:T(8,128)}, f32[128,8,128]{2,1,0:T(8,128)}, u32[]{:S(2)}, u32[]{:S(2)}) collective-permute-start(f32[128,8,128]{2,1,0:T(8,128)} %copy-done.4), channel_id=1, source_target_pairs={{0,16},{16,0},{32,48},{48,32},{64,80},{80,64},{96,112},{112,96},{1... | collective-permute-start | bytes 1572872 | tf_op jit(solution)/shard_map/ppermute | solution.py:235
  38.8 1.9 %copy-start = (f32[1024,768]{1,0:T(8,128)S(1)}, f32[1024,768]{1,0:T(8,128)}, u32[]{:S(2)}) copy-start(f32[1024,768]{1,0:T(8,128)} %vec_ref.1) | copy-start | bytes 9437188
  40.7 1.0 %copy-start.5 = (f32[128,8,128]{2,1,0:T(8,128)S(1)}, f32[128,8,128]{2,1,0:T(8,128)}, u32[]{:S(2)}) copy-start(f32[128,8,128]{2,1,0:T(8,128)} %copy-done.4) | copy-start | bytes 1572868
  49.5 1.7 %copy-start.1 = (f32[768,1024]{1,0:T(8,128)}, f32[768,1024]{1,0:T(8,128)S(1)}, u32[]{:S(2)}) copy-start(f32[768,1024]{1,0:T(8,128)S(1)} %get-tuple-element.10.vt_hbm) | copy-start | bytes 9437188
  51.2 1.7 %copy-start.2 = (f32[768,1024]{1,0:T(8,128)}, f32[768,1024]{1,0:T(8,128)S(1)}, u32[]{:S(2)}) copy-start(f32[768,1024]{1,0:T(8,128)S(1)} %get-tuple-element.11.wt_hbm) | copy-start | bytes 9437188
  52.9 1.7 %copy-start.3 = (bf16[48,256,128]{2,1,0:T(8,128)(2,1)}, bf16[48,256,128]{2,1,0:T(8,128)(2,1)S(1)}, u32[]{:S(2)}) copy-start(bf16[48,256,128]{2,1,0:T(8,128)(2,1)S(1)} %get-tuple-element.13.a_hbm) | copy-start | bytes 9437188

commit v5 on v4

v5 whole, which is shorter than its diff:
```python
import jax
import jax.numpy as jnp
from jax import lax
from jax.experimental import pallas as pl
from jax.experimental.pallas import tpu as pltpu
from jax.sharding import PartitionSpec as P

BOTH = ("row", "col")
LANES = 128
SPLITS = 64


def three_way(x):
    hi = x.astype(jnp.bfloat16).astype(jnp.float32)
    rest = x - hi
    mid = rest.astype(jnp.bfloat16).astype(jnp.float32)
    lo = (rest - mid).astype(jnp.bfloat16).astype(jnp.float32)
    return hi, mid, lo


KEPT = 4


def head_rows(ref, first, block):
    tiles = 6
    top = lax.broadcasted_iota(jnp.int32, (8, LANES), 0) < KEPT
    rows = []
    for e in range(16):
        at = (first + 2 * e) * 8 * tiles + block * 8
        even, odd = ref[at : at + 8, :], ref[at + 8 * tiles : at + 8 * tiles + 8, :]
        rows.append(jnp.where(top, even, pltpu.roll(odd, KEPT, axis=0)))
    return jnp.concatenate(rows, axis=0)


def tail_rows(ref, first, block):
    tiles = 6
    spots = [(first // 8 + e) * 8 * tiles + block * 8 for e in range(16)]
    return jnp.concatenate([ref[at : at + 8, :] for at in spots], axis=0)


def prep_kernel(
    core_ref, fill_ref, vec_ref, codes_ref, own_ref, sib_ref, vt_hbm, w_hbm, a_hbm, list_ref, vt_ref, w_ref, a_ref, tail_ref, sems
):
    core = core_ref[0]
    tiles = 6
    pairs = fill_ref.shape[0]
    rows = pairs * 8
    tail = rows // 2
    sublane = lax.broadcasted_iota(jnp.int32, (8, 256), 0)

    def no_row(i, carry):
        list_ref[i] = 0
        return carry

    def one_pair(d, at):
        for j in range(KEPT, 8):
            list_ref[at + j - KEPT] = d * (8 * tiles) + j
        return at + jnp.maximum(fill_ref[d] - KEPT, 0)

    lax.fori_loop(0, list_ref.shape[0], no_row, 0)
    lax.fori_loop(0, pairs, one_pair, 0)

    def some(i, carry):
        for k in range(32):
            row = vec_ref[pl.ds(list_ref[i * 32 + k], tiles, stride=8), :]
            tail_ref[pl.ds((i * 4 + k // 8) * (8 * tiles) + k % 8, tiles, stride=8), :] = row
        return carry

    lax.fori_loop(0, tail // 32, some, 0)
    for block in range(tiles):
        feats = slice(block * LANES, (block + 1) * LANES)
        for g in range(tail // LANES):
            vt_ref[feats, g * LANES : (g + 1) * LANES] = head_rows(vec_ref, g * 32, block).T
            vt_ref[feats, tail + g * LANES : tail + (g + 1) * LANES] = tail_rows(tail_ref, g * LANES, block).T
    sent = [pltpu.make_async_copy(vt_ref, vt_hbm, sems.at[0])]
    sent[0].start()

    def one_block(block, carry):
        codes = codes_ref[pl.ds(pl.multiple_of(block * 16, 16), 16), :]
        stack = []
        words_of = []
        for i in range(16):
            m = block * 16 + i
            shard, within = m // 6, m % 6
            half, j = within // 3, within % 3
            base = shard * 8 + j * 2
            mine = half == core
            words = []
            for h in range(2):
                spot = pl.ds(base + h, 8, stride=LANES)
                words.append(jnp.where(mine, own_ref[spot, :], sib_ref[spot, :]))
            words_of.append(words)
            both = jnp.concatenate(words, axis=1)
            norm = jnp.sum(both * both, axis=0, keepdims=True)
            hi, mid, lo = three_way(-2.0 * both)
            nhi, nmid, nlo = three_way(norm)
            norms = jnp.where(sublane == 0, nhi, jnp.where(sublane == 1, nmid, jnp.where(sublane == 2, nlo, 0.0)))
            stack += [hi, hi, hi, mid, mid, lo, norms, jnp.zeros_like(norms)]
            if i % 2 == 1:
                a_ref[m // 2] = jnp.concatenate(stack, axis=0).T.astype(jnp.bfloat16)
                stack = []
        for g in range(rows // LANES):
            cut = slice(g * LANES, (g + 1) * LANES)
            coded = []
            for i in range(16):
                code = jnp.broadcast_to(codes[i : i + 1, cut], (8, LANES))
                low = code & (LANES - 1)
                first = jnp.take_along_axis(words_of[i][0], low, axis=1, mode="promise_in_bounds")
                second = jnp.take_along_axis(words_of[i][1], low, axis=1, mode="promise_in_bounds")
                coded.append(jnp.where(code >= LANES, second, first))
            turned = jnp.concatenate(coded, axis=0).T
            for e in range(16):
                at = pl.ds(pl.multiple_of((g * 16 + e) * (8 * tiles) + block * 8, 8), 8)
                w_ref[at, :] = vec_ref[at, :] - turned[e * 8 : (e + 1) * 8, :]
        return carry

    lax.fori_loop(0, tiles, one_block, 0)
    sent += [
        pltpu.make_async_copy(w_ref, w_hbm, sems.at[1]),
        pltpu.make_async_copy(a_ref, a_hbm, sems.at[2]),
    ]
    for copy in sent[1:]:
        copy.start()
    for copy in sent:
        copy.wait()


PARTS = 8


def pick_kernel(start_ref, cent_ref, out_hbm, out_ref, sems):
    tiles = 6
    words = out_ref.shape[0] // PARTS
    slots = words // tiles
    copies = []
    for part in range(PARTS):

        def some(i, carry, part=part):
            for k in range(32):
                row = cent_ref[pl.ds(start_ref[part * slots + i * 32 + k], tiles, stride=8), :]
                out_ref[pl.ds(part * words + (i * 4 + k // 8) * (8 * tiles) + k % 8, tiles, stride=8), :] = row
            return carry

        lax.fori_loop(0, slots // 32, some, 0)
        cut = slice(part * words, (part + 1) * words)
        copies.append(pltpu.make_async_copy(out_ref.at[cut], out_hbm.at[cut], sems.at[part]))
        copies[-1].start()
    for copy in copies:
        copy.wait()


def tiled_view(x):
    n, w = x.shape
    return x.reshape(n // 8, 8, w // LANES, LANES).swapaxes(1, 2).reshape(n * w // LANES, LANES)


def untiled_view(x, n, w):
    return x.reshape(n // 8, w // LANES, 8, LANES).swapaxes(1, 2).reshape(n, w)


STAGES = ((0, 1), (1, 3), (3, 6))


def score_kernel(
    list_ref, count_ref, vt_hbm, w_hbm, cent_ref, a_hbm, pos_ref, live_ref, coded_ref, best_ref, vt_ref, w_ref, a_ref, tail_ref, acc_ref, part_ref, sems
):
    tiles = 6
    rows = pos_ref.shape[0] * LANES
    wide = 256
    head = rows // 2

    def fetch(k):
        lo, hi = STAGES[k]
        pairs, feats = slice(lo * 8, hi * 8), slice(lo * LANES, hi * LANES)
        copies = [
            pltpu.make_async_copy(a_hbm.at[pairs], a_ref.at[pairs], sems.at[k, 0]),
            pltpu.make_async_copy(vt_hbm.at[feats], vt_ref.at[feats], sems.at[k, 1]),
        ]
        if hi == tiles:
            copies.append(pltpu.make_async_copy(w_hbm, w_ref, sems.at[k, 2]))
        for copy in copies:
            copy.start()
        return copies

    def gather(first):
        for k in range(wide):
            row = cent_ref[pl.ds(list_ref[first + k], tiles, stride=8), :]
            tail_ref[pl.ds(k // 8 * (8 * tiles) + k % 8, tiles, stride=8), :] = row

    ones = jnp.ones((16, wide), jnp.bfloat16)
    none = jnp.zeros((SPLITS, wide), jnp.bfloat16)

    def score(block, t):
        cut = slice(t * wide, (t + 1) * wide)
        if t * wide < head:
            cent = [head_rows(cent_ref, t * 64 + g * 32, block).T for g in range(2)]
        else:
            cent = [tail_rows(tail_ref, g * LANES, block).T for g in range(2)]
        resid = vt_ref[block * LANES : (block + 1) * LANES, cut] - jnp.concatenate(cent, axis=1)
        least = jnp.zeros((1, wide), jnp.float32)
        for pair in range(8):
            left = a_ref[block * 8 + pair]
            for half in range(2):
                at = (pair * 2 + half) * 8
                top, mid, low = three_way(resid[at : at + 8, :])
                side = [
                    jnp.concatenate([top, mid], axis=0).astype(jnp.bfloat16),
                    jnp.concatenate([low, top], axis=0).astype(jnp.bfloat16),
                    jnp.concatenate([mid, top], axis=0).astype(jnp.bfloat16),
                    ones,
                ]
                side = [none] + side if half else side + [none]
                table = jnp.dot(left, jnp.concatenate(side, axis=0), preferred_element_type=jnp.float32)
                least += jnp.min(table, axis=0, keepdims=True)
        acc_ref[0:8, cut] += jnp.sum((resid * resid).reshape(16, 8, wide), axis=0)
        acc_ref[8:9, cut] += least

    waiting = [fetch(0)]
    acc_ref[...] = jnp.zeros_like(acc_ref)
    gather(0)
    for k, (lo, hi) in enumerate(STAGES):
        for copy in waiting[k]:
            copy.wait()
        if k == 0:
            waiting += [fetch(1), fetch(2)]
        for block in range(lo, hi):
            for t in range(3):
                score(block, t)
            if hi == tiles:
                share = rows // 8 // (hi - lo) + 1
                for d in range((block - lo) * share, min((block - lo + 1) * share, rows // 8)):
                    total = jnp.zeros((8, LANES), jnp.float32)
                    for b in range(tiles):
                        at = slice((d * tiles + b) * 8, (d * tiles + b + 1) * 8)
                        err = w_ref[at, :] - cent_ref[at, :]
                        total += err * err
                    part_ref[d * 8 : (d + 1) * 8, :] = total

    @pl.when(count_ref[0] > wide)
    def _():
        gather(wide)
        for block in range(tiles):
            score(block, 3)

    best = jnp.sum(acc_ref[0:8, :], axis=0, keepdims=True) + acc_ref[8:9, :]
    pos = pos_ref[...]
    live = live_ref[...] != 0
    found = jnp.zeros(pos.shape, jnp.float32)
    for h in range(rows // LANES):
        source = jnp.broadcast_to(best[:, h * LANES : (h + 1) * LANES], pos.shape)
        lane = jnp.take_along_axis(source, pos & (LANES - 1), axis=1, mode="promise_in_bounds")
        found = jnp.where(pos // LANES == h, lane, found)
    coded = [
        jnp.sum(part_ref[h * LANES : (h + 1) * LANES, :].T, axis=0, keepdims=True) for h in range(rows // LANES)
    ]
    coded_ref[...] = jnp.where(live, jnp.concatenate(coded, axis=0), 0.0)
    best_ref[...] = jnp.where(live, found, 0.0)


def pack_kernel(ids_hbm, book_hbm, lists_hbm, out_hbm, lists_ref, ids_ref, book_ref, out_ref, sems):
    fetches = [
        pltpu.make_async_copy(book_hbm, book_ref, sems.at[0]),
        pltpu.make_async_copy(ids_hbm, ids_ref, sems.at[1]),
        pltpu.make_async_copy(lists_hbm, lists_ref, sems.at[2]),
    ]
    for fetch in fetches:
        fetch.start()
    u = lax.axis_index("row")
    rows = ids_ref.shape[0]
    cols = out_ref.shape[0] // rows
    fetches[0].wait()
    fetches[1].wait()
    mine = book_ref[pl.ds(u, 12, stride=8), :]
    for r in range(rows):
        half = mine[(r % 2) * 6 : (r % 2) * 6 + 6, :]
        ids = ids_ref[r : r + 1, :].astype(jnp.float32)
        tile = jnp.concatenate([half, ids, ids], axis=0)
        out_ref[r * cols : (r + 1) * cols] = jnp.broadcast_to(tile[None], (cols, 8, LANES))
    send = pltpu.make_async_copy(out_ref, out_hbm, sems.at[3])
    send.start()
    fetches[2].wait()
    send.wait()


def pinned(x):
    return pltpu.with_memory_space_constraint(x, pltpu.HBM)


def local(vectors, list_ids, pq_codes, fill_counts, centroids, codebook):
    row_count = lax.axis_size("row")
    col_count = lax.axis_size("col")
    devices = row_count * col_count
    slots, width = vectors.shape
    cap = slots // devices
    subs = pq_codes.shape[1]
    f32 = jnp.float32
    my_row = lax.axis_index("row")
    core = my_row % 2

    per_row = LANES // cap
    vmem = pl.BlockSpec(memory_space=pltpu.VMEM)
    smem = pl.BlockSpec(memory_space=pltpu.SMEM)
    hbm = pl.BlockSpec(memory_space=pltpu.HBM)
    sent, lists = pl.pallas_call(
        pack_kernel,
        in_specs=[hbm, hbm, hbm],
        out_specs=[hbm, vmem],
        out_shape=[
            pltpu.HBM((devices, 8, LANES), f32),
            pltpu.VMEM((centroids.size // LANES, LANES), f32),
        ],
        scratch_shapes=[
            pltpu.VMEM((row_count, LANES), jnp.int32),
            pltpu.VMEM((codebook.size // LANES, LANES), f32),
            pltpu.VMEM((devices, 8, LANES), f32),
            pltpu.SemaphoreType.DMA((4,)),
        ],
        compiler_params=pltpu.CompilerParams(vmem_limit_bytes=4 << 20),
        name="pack",
    )(
        pinned(list_ids.reshape(row_count, LANES)),
        pinned(tiled_view(codebook.reshape(-1, codebook.shape[2]))),
        pinned(tiled_view(centroids)),
    )
    got = lax.all_to_all(sent, BOTH, 0, 0, tiled=True)
    sibling = lax.ppermute(got, "row", [(i, i ^ 1) for i in range(row_count)])

    me = my_row * col_count + lax.axis_index("col")
    want = lax.dynamic_slice(got[:, 6], (0, (me % per_row) * cap), (devices, cap))
    want = want.astype(jnp.int32).reshape(slots) % centroids.shape[0]
    start = (want // 8) * (8 * width // LANES) + want % 8
    picked = pl.pallas_call(
        pick_kernel,
        in_specs=[smem, vmem],
        out_specs=hbm,
        out_shape=pltpu.HBM((slots * width // LANES, LANES), f32),
        scratch_shapes=[pltpu.VMEM((slots * width // LANES, LANES), f32), pltpu.SemaphoreType.DMA((PARTS,))],
        compiler_params=pltpu.CompilerParams(vmem_limit_bytes=8 << 20),
        name="pick",
    )(start, lists)
    picked = untiled_view(picked, slots, width)
    cent = lax.all_to_all(picked.reshape(devices, cap, width), BOTH, 0, 0, tiled=True)
    cent = tiled_view(cent.reshape(slots, width))

    fill = fill_counts[0]
    extra = jnp.maximum(fill - KEPT, 0)
    pair = jnp.arange(devices, dtype=jnp.int32)
    before = jnp.sum(jnp.where(pair[None, :] < pair[:, None], extra[None, :], 0), axis=1)
    slot = jnp.arange(cap, dtype=jnp.int32)[None, :]
    pos = jnp.where(slot < KEPT, KEPT * pair[:, None] + slot, slots // 2 + before[:, None] + slot - KEPT)
    pos = pos.reshape(slots // LANES, LANES)
    live = (slot < fill[:, None]).astype(jnp.int32).reshape(slots // LANES, LANES)

    view = (slots * width // LANES, LANES)
    book = (subs // 2, 256, LANES)
    vt, w, a, rows = pl.pallas_call(
        prep_kernel,
        in_specs=[smem, smem, vmem, vmem, vmem, vmem],
        out_specs=[hbm] * 3 + [smem],
        out_shape=[
            pltpu.HBM((width, slots), f32),
            pltpu.HBM(view, f32),
            pltpu.HBM(book, jnp.bfloat16),
            jax.ShapeDtypeStruct((slots // 2 + 8,), jnp.int32),
        ],
        scratch_shapes=[
            pltpu.VMEM((width, slots), f32),
            pltpu.VMEM(view, f32),
            pltpu.VMEM(book, jnp.bfloat16),
            pltpu.VMEM((view[0] // 2, LANES), f32),
            pltpu.SemaphoreType.DMA((3,)),
        ],
        compiler_params=pltpu.CompilerParams(vmem_limit_bytes=32 << 20),
        name="prep",
    )(
        core.reshape(1).astype(jnp.int32),
        fill,
        tiled_view(vectors),
        pq_codes.T,
        got.reshape(devices * 8, LANES),
        sibling.reshape(devices * 8, LANES),
    )

    coded, best = pl.pallas_call(
        score_kernel,
        in_specs=[smem, smem, hbm, hbm, vmem, hbm, vmem, vmem],
        out_specs=[vmem] * 2,
        out_shape=[jax.ShapeDtypeStruct((slots // LANES, LANES), f32)] * 2,
        scratch_shapes=[
            pltpu.VMEM((width, slots), f32),
            pltpu.VMEM(view, f32),
            pltpu.VMEM(book, jnp.bfloat16),
            pltpu.VMEM((view[0] // 4, LANES), f32),
            pltpu.VMEM((16, slots), f32),
            pltpu.VMEM((slots, LANES), f32),
            pltpu.SemaphoreType.DMA((len(STAGES), 3)),
        ],
        compiler_params=pltpu.CompilerParams(vmem_limit_bytes=32 << 20),
        name="score",
    )(rows, jnp.sum(extra).reshape(1), pinned(vt), pinned(w), cent, pinned(a), pos, live)
    return coded.reshape(slots), best.reshape(slots)


def solution(mesh):
    in_specs = (
        P(BOTH, None),
        P(BOTH),
        P(BOTH, None),
        P(BOTH, None),
        P(BOTH, None),
        P("col", None, None),
    )
    out_specs = (P(BOTH), P(BOTH))
    return jax.shard_map(local, mesh=mesh, in_specs=in_specs, out_specs=out_specs, check_vma=False)
```

time: 92.9 us -> 91.5 us (0.985)
  waiting for transfers between devices: 36 us -> 20.5 us
  Pallas kernels: 28.3 us -> 36.1 us
  local copies, waits for them, and re-layouts: 9.07 us -> 13.1 us
  other arithmetic: 0.98 us -> 3.08 us
    all_to_all x1, waiting for transfers between devices: 21.9 us -> 6.71 us  [local(): lax.all_to_all(picked.reshape(devices, cap, width), BOTH, 0, 0, tiled=True)]
    pallas_call x2, Pallas kernels: 23.6 us -> 31.4 us  [the longest x1 17.1 us: local(): pl.pallas_call(prep_kernel, in_specs=[smem, smem, vmem, vmem, vmem, vmem]...]
    add x0 -> x7, local copies, waits for them, and re-layouts: none -> 5.83 us  [the longest x3 3.59 us: local(): slots // 2 + before[:, None] + slot - KEPT]
    unnamed x16 -> x11, local copies, waits for them, and re-layouts: 7.98 us -> 3.45 us
    lt x0 -> x3, local copies, waits for them, and re-layouts: none -> 2.99 us  [local(): slot < fill[:, None]]
    convert_element_type x1 -> x0, local copies, waits for them, and re-layouts: 0.94 us -> none  [local(): (slot_pos[None, :] < fill_counts[0][:, None]).astype(jnp.int32)]
  transfers between devices with their start and end apart: 3 -> 3, of which waited for: 3 -> 2; matrix products, arithmetic and copies ran while one was open for 2% -> 14% of each run, Pallas kernels for 8% -> 19%
where the time goes in v5:
time: 91.5 us; the launch traced here: 90.8 us
  Pallas kernels  36.1 us (39%)
  waiting for transfers between devices  20.5 us (22%)
  starting transfers between devices  17.1 us (19%)
  local copies, waits for them, and re-layouts  13.1 us (14%)
  other arithmetic  3.08 us (3%)
  between operations  0.94 us (1%)
    pallas_call x1, Pallas kernels, local(): pl.pallas_call(prep_kernel, in_specs=[smem, smem, vmem, vmem, vmem, vmem]...  17.1 us
    pallas_call x1, Pallas kernels, local(): pl.pallas_call(score_kernel, in_specs=[smem, smem, hbm, hbm, vmem, hbm, v...  14.2 us
    all_to_all x1, waiting for transfers between devices, local(): got = lax.all_to_all(sent, BOTH, 0, 0, tiled=True)  13.8 us
    all_to_all x1, starting transfers between devices, local(): got = lax.all_to_all(sent, BOTH, 0, 0, tiled=True)  11.5 us
    all_to_all x1, waiting for transfers between devices, local(): lax.all_to_all(picked.reshape(devices, cap, width), BOTH, 0, 0, tiled=True)  6.71 us
    all_to_all x1, starting transfers between devices, local(): lax.all_to_all(picked.reshape(devices, cap, width), BOTH, 0, 0, tiled=True)  4.41 us
    add x3, local copies, waits for them, and re-layouts, local(): slots // 2 + before[:, None] + slot - KEPT  3.59 us
    unnamed x11, local copies, waits for them, and re-layouts  3.45 us
  transfers between devices with their start and end apart: 3, of which 2 were waited for; matrix products, arithmetic and copies ran while one was open for 14% of the time, Pallas kernels for 19%

profile of v5, /device:TPU:1, one launch (start us, length us, event | category | flops | bytes accessed | tf_op | source)
XLA Modules:
  0.0 90.8 jit_solution(6898574811733732862)
XLA Ops:
  0.6 1.7 %pack.1 = (f32[128,8,128]{2,1,0:T(8,128)}, f32[3072,128]{1,0:T(8,128)S(1)}) custom-call(s32[8,128]{1,0:T(8,128)} %bitcast.46, f32[96,128]{1,0:T(8,128)} %bitcast.45, f32[3072,128]{1,0:T(8,128)} %bitcast.44), custom_call_target="tpu_custom_call" | custom-call | tf_op jit(solution)/shard_map/pack/pallas_call | solution.py:304
  2.3 11.5 %all-to-all-start = ((f32[128,8,128]{2,1,0:T(8,128)}), f32[128,8,128]{2,1,0:T(8,128)S(1)}, u32[]{:S(2)}, u32[]{:S(2)}) async-start(f32[128,8,128]{2,1,0:T(8,128)} %get-tuple-element.10), calls=%async_computation | async-start | bytes 1048576 | tf_op jit(solution)/shard_map/all_to_all | solution.py:325
  13.8 13.8 %all-to-all-done = f32[128,8,128]{2,1,0:T(8,128)S(1)} async-done(((f32[128,8,128]{2,1,0:T(8,128)}), f32[128,8,128]{2,1,0:T(8,128)S(1)}, u32[]{:S(2)}, u32[]{:S(2)}) %all-to-all-start) | async-done | bytes 524320 | tf_op jit(solution)/shard_map/all_to_all | solution.py:325
  28.1 3.0 %pick.1 = f32[6144,128]{1,0:T(8,128)} custom-call(s32[1024]{0:T(1024)S(1)} %fusion.2.start_ref, f32[3072,128]{1,0:T(8,128)S(1)} %get-tuple-element.14.cent_ref), custom_call_target="tpu_custom_call" | custom-call | tf_op jit(solution)/shard_map/pick/pallas_call | solution.py:332
  31.2 4.4 %all-to-all-start.1 = ((f32[128,8,768]{2,1,0:T(8,128)}), f32[128,8,768]{2,1,0:T(8,128)S(1)}, u32[]{:S(2)}, u32[]{:S(2)}) async-start(f32[128,8,768]{2,1,0:T(8,128)} %bitcast.43), calls=%async_computation.1 | async-start | bytes 6291456 | tf_op jit(solution)/shard_map/all_to_all | solution.py:342
  35.6 0.7 broadcast_in_dim.33
  36.8 0.7 fusion.7
  37.6 0.7 add.107
  38.3 0.7 lt.69
  39.6 0.7 add.99
  40.3 0.9 %add.100 = s32[8,128]{1,0:T(8,128)S(1)} reshape(s32[8,16,8]{2,1,0:T(8,128)} %add.99) | data formatting | bytes 8192 | tf_op jit(solution)/shard_map/add | solution.py:350
  41.2 1.4 %lt.70 = s32[8,16,8]{2,1,0:T(8,128)} broadcast(s32[8,16]{1,0:T(8,128)} %lt.69), dimensions={0,1} | broadcast | bytes 4608 | tf_op jit(solution)/shard_map/lt | solution.py:352
  42.6 0.9 %lt.71 = s32[8,128]{1,0:T(8,128)S(1)} reshape(s32[8,16,8]{2,1,0:T(8,128)} %lt.70) | data formatting | bytes 8192 | tf_op jit(solution)/shard_map/lt | solution.py:352
  43.5 1.4 %add.108 = s32[8,16,8]{2,1,0:T(8,128)} broadcast(s32[8,16]{1,0:T(8,128)} %add.107), dimensions={0,1} | broadcast | bytes 4608 | tf_op jit(solution)/shard_map/add | solution.py:350
  44.9 1.5 %add.109 = s32[8,128]{1,0:T(8,128)} reshape(s32[8,16,8]{2,1,0:T(8,128)} %add.108) | data formatting | bytes 8192 | tf_op jit(solution)/shard_map/add | solution.py:350
  46.4 1.2 %collective-permute-start = (f32[128,8,128]{2,1,0:T(8,128)}, f32[128,8,128]{2,1,0:T(8,128)S(1)}, u32[]{:S(2)}, u32[]{:S(2)}) collective-permute-start(f32[128,8,128]{2,1,0:T(8,128)} %copy-done.1), channel_id=1, source_target_pairs={{0,16},{16,0},{32,48},{48,32},{64,80},{80,64},{96,112},{112,96},{1... | collective-permute-start | bytes 1572872 | tf_op jit(solution)/shard_map/ppermute | solution.py:326
  47.6 0.7 maximum_reduce_fusion
  48.3 0.6 compare_convert_fusion.live_ref
  48.9 0.7 add_select_fusion.3.pos_ref
  49.7 1.9 %copy-done = f32[1024,768]{1,0:T(8,128)S(1)} copy-done((f32[1024,768]{1,0:T(8,128)S(1)}, f32[1024,768]{1,0:T(8,128)}, u32[]{:S(2)}) %copy-start) | copy-done | bytes 3145752
  51.5 1.0 %copy-done.2 = f32[128,8,128]{2,1,0:T(8,128)S(1)} copy-done((f32[128,8,128]{2,1,0:T(8,128)S(1)}, f32[128,8,128]{2,1,0:T(8,128)}, u32[]{:S(2)}) %copy-start.2) | copy-done | bytes 524312
  52.6 17.1 %prep.1 = (f32[768,1024]{1,0:T(8,128)}, f32[6144,128]{1,0:T(8,128)}, bf16[48,256,128]{2,1,0:T(8,128)(2,1)}, s32[520]{0:T(1024)S(1)}) custom-call(s32[1]{0:T(128)} %bitcast.core_ref, s32[128]{0:T(128)S(1)} %bitcast.42, f32[6144,128]{1,0:T(8,128)S(1)} %bitcast.38, s32[96,1024]{1,0:T(8,128)S(1)} %bitcast.41, f32[1024,128]{1,0:T(8,128)S(1)} %bitcast.39, ...), custom_call_target="tpu_custom_call" | custom-call | tf_op jit(solution)/shard_map/prep/pallas_call | solution.py:356
  69.7 6.7 %all-to-all-done.1 = f32[128,8,768]{2,1,0:T(8,128)S(1)} async-done(((f32[128,8,768]{2,1,0:T(8,128)}), f32[128,8,768]{2,1,0:T(8,128)S(1)}, u32[]{:S(2)}, u32[]{:S(2)}) %all-to-all-start.1) | async-done | bytes 3145760 | tf_op jit(solution)/shard_map/all_to_all | solution.py:342
  76.4 14.2 %score.1 = (f32[8,128]{1,0:T(8,128)}, f32[8,128]{1,0:T(8,128)}) custom-call(s32[520]{0:T(1024)S(1)} %get-tuple-element.11.list_ref, s32[1]{0:T(128)} %bitcast.15.count_ref, f32[768,1024]{1,0:T(8,128)} %get-tuple-element.12.vt_hbm, f32[6144,128]{1,0:T(8,128)} %get-tuple-element.13.w_hbm, f32[6144,128]{1,0:T(8,128)S(1)} %bitcast.37, ...), custom_call_target="tpu_custom_call" | custom-call | tf_op jit(solution)/shard_map/score/pallas_call | solution.py:384
  (21 shorter events, 1.7 us)
Async XLA Ops:
  2.3 25.4 %all-to-all-start = ((f32[128,8,128]{2,1,0:T(8,128)}), f32[128,8,128]{2,1,0:T(8,128)S(1)}, u32[]{:S(2)}, u32[]{:S(2)}) async-start(f32[128,8,128]{2,1,0:T(8,128)} %get-tuple-element.10), calls=%async_computation | async-start | bytes 1048576 | tf_op jit(solution)/shard_map/all_to_all | solution.py:325
  27.7 3.5 %copy-start.1 = (f32[128,8,128]{2,1,0:T(8,128)}, f32[128,8,128]{2,1,0:T(8,128)S(1)}, u32[]{:S(2)}) copy-start(f32[128,8,128]{2,1,0:T(8,128)S(1)} %all-to-all-done) | copy-start | bytes 1572868
  31.1 5.7 %copy-start.4 = (s32[1,128]{1,0:T(1,128)S(1)}, s32[1,128]{1,0:T(1,128)}, u32[]{:S(2)}) copy-start(s32[1,128]{1,0:T(1,128)} %param.9) | copy-start | bytes 1540
  31.1 18.5 %copy-start.3 = (s32[1024,96]{0,1:T(8,128)S(1)}, s32[1024,96]{0,1:T(8,128)}, u32[]{:S(2)}) copy-start(s32[1024,96]{0,1:T(8,128)} %param.8) | copy-start | bytes 1179652
  31.2 45.3 %all-to-all-start.1 = ((f32[128,8,768]{2,1,0:T(8,128)}), f32[128,8,768]{2,1,0:T(8,128)S(1)}, u32[]{:S(2)}, u32[]{:S(2)}) async-start(f32[128,8,768]{2,1,0:T(8,128)} %bitcast.43), calls=%async_computation.1 | async-start | bytes 6291456 | tf_op jit(solution)/shard_map/all_to_all | solution.py:342
  46.4 3.2 %collective-permute-start = (f32[128,8,128]{2,1,0:T(8,128)}, f32[128,8,128]{2,1,0:T(8,128)S(1)}, u32[]{:S(2)}, u32[]{:S(2)}) collective-permute-start(f32[128,8,128]{2,1,0:T(8,128)} %copy-done.1), channel_id=1, source_target_pairs={{0,16},{16,0},{32,48},{48,32},{64,80},{80,64},{96,112},{112,96},{1... | collective-permute-start | bytes 1572872 | tf_op jit(solution)/shard_map/ppermute | solution.py:326
  49.6 1.9 %copy-start = (f32[1024,768]{1,0:T(8,128)S(1)}, f32[1024,768]{1,0:T(8,128)}, u32[]{:S(2)}) copy-start(f32[1024,768]{1,0:T(8,128)} %param.6) | copy-start | bytes 9437188
  51.5 1.0 %copy-start.2 = (f32[128,8,128]{2,1,0:T(8,128)S(1)}, f32[128,8,128]{2,1,0:T(8,128)}, u32[]{:S(2)}) copy-start(f32[128,8,128]{2,1,0:T(8,128)} %copy-done.1) | copy-start | bytes 1572868

commit v6 on v5

--- a/solution.py
+++ b/solution.py
@@ -39,7 +39,8 @@
 
 
 def prep_kernel(
-    core_ref, fill_ref, vec_ref, codes_ref, own_ref, sib_ref, vt_hbm, w_hbm, a_hbm, list_ref, vt_ref, w_ref, a_ref, tail_ref, sems
+    core_ref, fill_ref, fills_ref, vec_ref, codes_ref, own_ref, sib_ref, vt_hbm, w_hbm, a_hbm, list_hbm, pos_ref, live_ref,
+    list_ref, vt_ref, w_ref, a_ref, tail_ref, sems
 ):
     core = core_ref[0]
     tiles = 6
@@ -57,8 +58,23 @@
             list_ref[at + j - KEPT] = d * (8 * tiles) + j
         return at + jnp.maximum(fill_ref[d] - KEPT, 0)
 
-    lax.fori_loop(0, list_ref.shape[0], no_row, 0)
-    lax.fori_loop(0, pairs, one_pair, 0)
+    lax.fori_loop(0, tail, no_row, 0)
+    list_ref[list_ref.shape[0] - 1] = lax.fori_loop(0, pairs, one_pair, 0)
+    sent = [pltpu.make_async_copy(list_ref, list_hbm, sems.at[3])]
+    sent[0].start()
+
+    across = lax.broadcasted_iota(jnp.int32, (pairs, pairs), 1)
+    down = lax.broadcasted_iota(jnp.int32, (pairs, pairs), 0)
+    spot = lax.broadcasted_iota(jnp.int32, pos_ref.shape, 0) * LANES + lax.broadcasted_iota(jnp.int32, pos_ref.shape, 1)
+    slot = spot % 8
+    fills = jnp.broadcast_to(fills_ref[...], pos_ref.shape)
+    extra = jnp.maximum(fills - KEPT, 0).astype(jnp.float32).astype(jnp.bfloat16)
+    earlier = jnp.where(down < across, 1.0, 0.0).astype(jnp.bfloat16)
+    before = jnp.dot(extra, earlier, preferred_element_type=jnp.float32).astype(jnp.int32)
+    fill_of = jnp.take_along_axis(fills, spot // 8, axis=1, mode="promise_in_bounds")
+    before_of = jnp.take_along_axis(before, spot // 8, axis=1, mode="promise_in_bounds")
+    pos_ref[...] = jnp.where(slot < KEPT, KEPT * (spot // 8) + slot, tail + before_of + slot - KEPT)
+    live_ref[...] = (slot < fill_of).astype(jnp.int32)
 
     def some(i, carry):
         for k in range(32):
@@ -72,8 +88,8 @@
         for g in range(tail // LANES):
             vt_ref[feats, g * LANES : (g + 1) * LANES] = head_rows(vec_ref, g * 32, block).T
             vt_ref[feats, tail + g * LANES : tail + (g + 1) * LANES] = tail_rows(tail_ref, g * LANES, block).T
-    sent = [pltpu.make_async_copy(vt_ref, vt_hbm, sems.at[0])]
-    sent[0].start()
+    sent.append(pltpu.make_async_copy(vt_ref, vt_hbm, sems.at[0]))
+    sent[1].start()
 
     def one_block(block, carry):
         codes = codes_ref[pl.ds(pl.multiple_of(block * 16, 16), 16), :]
@@ -119,7 +135,7 @@
         pltpu.make_async_copy(w_ref, w_hbm, sems.at[1]),
         pltpu.make_async_copy(a_ref, a_hbm, sems.at[2]),
     ]
-    for copy in sent[1:]:
+    for copy in sent[2:]:
         copy.start()
     for copy in sent:
         copy.wait()
@@ -162,20 +178,24 @@
 
 
 def score_kernel(
-    list_ref, count_ref, vt_hbm, w_hbm, cent_ref, a_hbm, pos_ref, live_ref, coded_ref, best_ref, vt_ref, w_ref, a_ref, tail_ref, acc_ref, part_ref, sems
+    list_hbm, vt_hbm, w_hbm, cent_ref, a_hbm, pos_ref, live_ref, coded_ref, best_ref,
+    list_ref, vt_ref, w_ref, a_ref, tail_ref, acc_ref, part_ref, sems
 ):
     tiles = 6
     rows = pos_ref.shape[0] * LANES
     wide = 256
     head = rows // 2
+    sure = slice(0, head + wide)
 
     def fetch(k):
         lo, hi = STAGES[k]
         pairs, feats = slice(lo * 8, hi * 8), slice(lo * LANES, hi * LANES)
         copies = [
             pltpu.make_async_copy(a_hbm.at[pairs], a_ref.at[pairs], sems.at[k, 0]),
-            pltpu.make_async_copy(vt_hbm.at[feats], vt_ref.at[feats], sems.at[k, 1]),
+            pltpu.make_async_copy(vt_hbm.at[feats, sure], vt_ref.at[feats, sure], sems.at[k, 1]),
         ]
+        if k == 0:
+            copies.append(pltpu.make_async_copy(list_hbm, list_ref, sems.at[k, 2]))
         if hi == tiles:
             copies.append(pltpu.make_async_copy(w_hbm, w_ref, sems.at[k, 2]))
         for copy in copies:
@@ -215,16 +235,17 @@
         acc_ref[0:8, cut] += jnp.sum((resid * resid).reshape(16, 8, wide), axis=0)
         acc_ref[8:9, cut] += least
 
-    waiting = [fetch(0)]
+    waiting = fetch(0)
     acc_ref[...] = jnp.zeros_like(acc_ref)
-    gather(0)
     for k, (lo, hi) in enumerate(STAGES):
-        for copy in waiting[k]:
+        for copy in waiting:
             copy.wait()
-        if k == 0:
-            waiting += [fetch(1), fetch(2)]
+        if k + 1 < len(STAGES):
+            waiting = fetch(k + 1)
         for block in range(lo, hi):
             for t in range(3):
+                if block == 0 and t == 2:
+                    gather(0)
                 score(block, t)
             if hi == tiles:
                 share = rows // 8 // (hi - lo) + 1
@@ -236,9 +257,13 @@
                         total += err * err
                     part_ref[d * 8 : (d + 1) * 8, :] = total
 
-    @pl.when(count_ref[0] > wide)
+    @pl.when(list_ref[list_ref.shape[0] - 1] > wide)
     def _():
+        rest = slice(sure.stop, rows)
+        last = pltpu.make_async_copy(vt_hbm.at[:, rest], vt_ref.at[:, rest], sems.at[0, 0])
+        last.start()
         gather(wide)
+        last.wait()
         for block in range(tiles):
             score(block, 3)
 
@@ -342,39 +367,34 @@
     cent = lax.all_to_all(picked.reshape(devices, cap, width), BOTH, 0, 0, tiled=True)
     cent = tiled_view(cent.reshape(slots, width))
 
-    fill = fill_counts[0]
-    extra = jnp.maximum(fill - KEPT, 0)
-    pair = jnp.arange(devices, dtype=jnp.int32)
-    before = jnp.sum(jnp.where(pair[None, :] < pair[:, None], extra[None, :], 0), axis=1)
-    slot = jnp.arange(cap, dtype=jnp.int32)[None, :]
-    pos = jnp.where(slot < KEPT, KEPT * pair[:, None] + slot, slots // 2 + before[:, None] + slot - KEPT)
-    pos = pos.reshape(slots // LANES, LANES)
-    live = (slot < fill[:, None]).astype(jnp.int32).reshape(slots // LANES, LANES)
-
     view = (slots * width // LANES, LANES)
     book = (subs // 2, 256, LANES)
-    vt, w, a, rows = pl.pallas_call(
+    vt, w, a, rows, pos, live = pl.pallas_call(
         prep_kernel,
-        in_specs=[smem, smem, vmem, vmem, vmem, vmem],
-        out_specs=[hbm] * 3 + [smem],
+        in_specs=[smem, smem, vmem, vmem, vmem, vmem, vmem],
+        out_specs=[hbm] * 4 + [vmem] * 2,
         out_shape=[
             pltpu.HBM((width, slots), f32),
             pltpu.HBM(view, f32),
             pltpu.HBM(book, jnp.bfloat16),
-            jax.ShapeDtypeStruct((slots // 2 + 8,), jnp.int32),
+            pltpu.HBM((slots,), jnp.int32),
+            jax.ShapeDtypeStruct((slots // LANES, LANES), jnp.int32),
+            jax.ShapeDtypeStruct((slots // LANES, LANES), jnp.int32),
         ],
         scratch_shapes=[
+            pltpu.SMEM((slots,), jnp.int32),
             pltpu.VMEM((width, slots), f32),
             pltpu.VMEM(view, f32),
             pltpu.VMEM(book, jnp.bfloat16),
             pltpu.VMEM((view[0] // 2, LANES), f32),
-            pltpu.SemaphoreType.DMA((3,)),
+            pltpu.SemaphoreType.DMA((4,)),
         ],
         compiler_params=pltpu.CompilerParams(vmem_limit_bytes=32 << 20),
         name="prep",
     )(
         core.reshape(1).astype(jnp.int32),
-        fill,
+        fill_counts[0],
+        fill_counts,
         tiled_view(vectors),
         pq_codes.T,
         got.reshape(devices * 8, LANES),
@@ -383,10 +403,11 @@
 
     coded, best = pl.pallas_call(
         score_kernel,
-        in_specs=[smem, smem, hbm, hbm, vmem, hbm, vmem, vmem],
+        in_specs=[hbm, hbm, hbm, vmem, hbm, vmem, vmem],
         out_specs=[vmem] * 2,
         out_shape=[jax.ShapeDtypeStruct((slots // LANES, LANES), f32)] * 2,
         scratch_shapes=[
+            pltpu.SMEM((slots,), jnp.int32),
             pltpu.VMEM((width, slots), f32),
             pltpu.VMEM(view, f32),
             pltpu.VMEM(book, jnp.bfloat16),
@@ -397,7 +418,7 @@
         ],
         compiler_params=pltpu.CompilerParams(vmem_limit_bytes=32 << 20),
         name="score",
-    )(rows, jnp.sum(extra).reshape(1), pinned(vt), pinned(w), cent, pinned(a), pos, live)
+    )(pinned(rows), pinned(vt), pinned(w), cent, pinned(a), pos, live)
     return coded.reshape(slots), best.reshape(slots)
 
 

time: 91.5 us -> 90.2 us (0.986)
  waiting for transfers between devices: 20.5 us -> 33.1 us
  local copies, waits for them, and re-layouts: 13.1 us -> 3.1 us
  other arithmetic: 3.08 us -> 0.29 us
    all_to_all x1, waiting for transfers between devices: 6.71 us -> 17.4 us  [local(): lax.all_to_all(picked.reshape(devices, cap, width), BOTH, 0, 0, tiled=True)]
    add x7 -> x0, local copies, waits for them, and re-layouts: 5.83 us -> none  [the longest x3 3.59 us: local(): slots // 2 + before[:, None] + slot - KEPT]
    lt x3 -> x0, local copies, waits for them, and re-layouts: 2.99 us -> none  [local(): slot < fill[:, None]]
    ppermute x1, waiting for transfers between devices: 0.01 us -> 1.88 us  [local(): sibling = lax.ppermute(got, 'row', [(i, i ^ 1) for i in range(row_count)])]
    unnamed x11 -> x10, local copies, waits for them, and re-layouts: 3.45 us -> 2.95 us
  transfers between devices with their start and end apart: 3 -> 3, of which waited for: 2 -> 3; matrix products, arithmetic and copies ran while one was open for 14% -> 0% of each run, Pallas kernels for 19% -> 19%
where the time goes in v6:
time: 90.2 us; the launch traced here: 89.8 us
  Pallas kernels  35.2 us (39%)
  waiting for transfers between devices  33.1 us (37%)
  starting transfers between devices  17.2 us (19%)
  local copies, waits for them, and re-layouts  3.1 us (3%)
    all_to_all x1, waiting for transfers between devices, local(): lax.all_to_all(picked.reshape(devices, cap, width), BOTH, 0, 0, tiled=True)  17.4 us
    pallas_call x1, Pallas kernels, local(): pl.pallas_call(prep_kernel, in_specs=[smem, smem, vmem, vmem, vmem, vmem,...  17.3 us
    all_to_all x1, waiting for transfers between devices, local(): got = lax.all_to_all(sent, BOTH, 0, 0, tiled=True)  13.8 us
    pallas_call x1, Pallas kernels, local(): pl.pallas_call(score_kernel, in_specs=[hbm, hbm, hbm, vmem, hbm, vmem, vm...  13.2 us
    all_to_all x1, starting transfers between devices, local(): got = lax.all_to_all(sent, BOTH, 0, 0, tiled=True)  11.5 us
    all_to_all x1, starting transfers between devices, local(): lax.all_to_all(picked.reshape(devices, cap, width), BOTH, 0, 0, tiled=True)  4.41 us
    pallas_call x1, Pallas kernels, local(): pl.pallas_call(pick_kernel, in_specs=[smem, vmem], out_specs=hbm, out_sha...  3.03 us
    unnamed x10, local copies, waits for them, and re-layouts  2.95 us
  transfers between devices with their start and end apart: 3, of which 3 were waited for; matrix products, arithmetic and copies ran while one was open for 0% of the time, Pallas kernels for 19%

profile of v6, /device:TPU:1, one launch (start us, length us, event | category | flops | bytes accessed | tf_op | source)
XLA Modules:
  0.0 89.8 jit_solution(13651863587623157162)
XLA Ops:
  0.6 1.7 %pack.1 = (f32[128,8,128]{2,1,0:T(8,128)}, f32[3072,128]{1,0:T(8,128)S(1)}) custom-call(s32[8,128]{1,0:T(8,128)} %bitcast.41, f32[96,128]{1,0:T(8,128)} %bitcast.40, f32[3072,128]{1,0:T(8,128)} %bitcast.39), custom_call_target="tpu_custom_call" | custom-call | tf_op jit(solution)/shard_map/pack/pallas_call | solution.py:329
  2.3 11.5 %all-to-all-start = ((f32[128,8,128]{2,1,0:T(8,128)}), f32[128,8,128]{2,1,0:T(8,128)S(1)}, u32[]{:S(2)}, u32[]{:S(2)}) async-start(f32[128,8,128]{2,1,0:T(8,128)} %get-tuple-element.12), calls=%async_computation | async-start | bytes 1048576 | tf_op jit(solution)/shard_map/all_to_all | solution.py:350
  13.8 13.8 %all-to-all-done = f32[128,8,128]{2,1,0:T(8,128)S(1)} async-done(((f32[128,8,128]{2,1,0:T(8,128)}), f32[128,8,128]{2,1,0:T(8,128)S(1)}, u32[]{:S(2)}, u32[]{:S(2)}) %all-to-all-start) | async-done | bytes 524320 | tf_op jit(solution)/shard_map/all_to_all | solution.py:350
  27.7 0.0 copy-start.1
  27.7 0.1 slice.4
  27.7 0.3 convert_reduce_fusion
  28.0 0.1 convert_element_type.8
  28.1 3.0 %pick.1 = f32[6144,128]{1,0:T(8,128)} custom-call(s32[1024]{0:T(1024)S(1)} %fusion.2.start_ref, f32[3072,128]{1,0:T(8,128)S(1)} %get-tuple-element.16.cent_ref), custom_call_target="tpu_custom_call" | custom-call | tf_op jit(solution)/shard_map/pick/pallas_call | solution.py:357
  31.1 0.0 copy-start.3
  31.2 0.0 copy-start.4
  31.2 0.0 copy-done.1
  31.2 4.4 %all-to-all-start.1 = ((f32[128,8,768]{2,1,0:T(8,128)}), f32[128,8,768]{2,1,0:T(8,128)S(1)}, u32[]{:S(2)}, u32[]{:S(2)}) async-start(f32[128,8,768]{2,1,0:T(8,128)} %bitcast.38), calls=%async_computation.1 | async-start | bytes 6291456 | tf_op jit(solution)/shard_map/all_to_all | solution.py:367
  35.6 1.3 %collective-permute-start = (f32[128,8,128]{2,1,0:T(8,128)}, f32[128,8,128]{2,1,0:T(8,128)}, u32[]{:S(2)}, u32[]{:S(2)}) collective-permute-start(f32[128,8,128]{2,1,0:T(8,128)} %copy-done.1), channel_id=1, source_target_pairs={{0,16},{16,0},{32,48},{48,32},{64,80},{80,64},{96,112},{112,96},{1... | collective-permute-start | bytes 1572872 | tf_op jit(solution)/shard_map/ppermute | solution.py:351
  36.9 1.9 %collective-permute-done = f32[128,8,128]{2,1,0:T(8,128)} collective-permute-done((f32[128,8,128]{2,1,0:T(8,128)}, f32[128,8,128]{2,1,0:T(8,128)}, u32[]{:S(2)}, u32[]{:S(2)}) %collective-permute-start) | collective-permute-done | bytes 524320 | tf_op jit(solution)/shard_map/ppermute | solution.py:351
  38.8 0.0 copy-done.3
  38.8 0.0 copy-done.4
  38.8 0.0 copy-start
  38.8 1.9 %copy-done = f32[1024,768]{1,0:T(8,128)S(1)} copy-done((f32[1024,768]{1,0:T(8,128)S(1)}, f32[1024,768]{1,0:T(8,128)}, u32[]{:S(2)}) %copy-start) | copy-done | bytes 3145752
  40.7 0.0 copy-start.2
  40.7 1.0 %copy-done.2 = f32[128,8,128]{2,1,0:T(8,128)S(1)} copy-done((f32[128,8,128]{2,1,0:T(8,128)S(1)}, f32[128,8,128]{2,1,0:T(8,128)}, u32[]{:S(2)}) %copy-start.2) | copy-done | bytes 524312
  41.7 17.3 %prep.1 = (f32[768,1024]{1,0:T(8,128)}, f32[6144,128]{1,0:T(8,128)}, bf16[48,256,128]{2,1,0:T(8,128)(2,1)}, s32[1024]{0:T(1024)}, s32[8,128]{1,0:T(8,128)S(1)}, /*index=5*/s32[8,128]{1,0:T(8,128)S(1)}) custom-call(s32[1]{0:T(128)} %bitcast.core_ref, s32[128]{0:T(128)S(1)} %bitcast.37, s32[1,128]{1,0:T(1,128)S(1)} %copy-done.4, f32[6144,128]{1,0:T(8,128)S(1)} %bitcast.34, ...), custom_call_target="tpu_custom_call" | custom-call | tf_op jit(solution)/shard_map/prep/pallas_call | solution.py:372
  59.0 17.4 %all-to-all-done.1 = f32[128,8,768]{2,1,0:T(8,128)S(1)} async-done(((f32[128,8,768]{2,1,0:T(8,128)}), f32[128,8,768]{2,1,0:T(8,128)S(1)}, u32[]{:S(2)}, u32[]{:S(2)}) %all-to-all-start.1) | async-done | bytes 3145760 | tf_op jit(solution)/shard_map/all_to_all | solution.py:367
  76.4 13.2 %score.1 = (f32[8,128]{1,0:T(8,128)}, f32[8,128]{1,0:T(8,128)}) custom-call(s32[1024]{0:T(1024)} %get-tuple-element.13.list_hbm, f32[768,1024]{1,0:T(8,128)} %get-tuple-element.14.vt_hbm, f32[6144,128]{1,0:T(8,128)} %get-tuple-element.15.w_hbm, f32[6144,128]{1,0:T(8,128)S(1)} %bitcast.33, bf16[48,256,128]{2,1,0:T(8,128)(2,1)} %get-tuple-element.17.a_hbm, ...), custom_call_target="tpu_custom_call" | custom-call | tf_op jit(solution)/shard_map/score/pallas_call | solution.py:404
  (1 shorter events, 0.0 us)
Async XLA Ops:
  2.3 25.4 %all-to-all-start = ((f32[128,8,128]{2,1,0:T(8,128)}), f32[128,8,128]{2,1,0:T(8,128)S(1)}, u32[]{:S(2)}, u32[]{:S(2)}) async-start(f32[128,8,128]{2,1,0:T(8,128)} %get-tuple-element.12), calls=%async_computation | async-start | bytes 1048576 | tf_op jit(solution)/shard_map/all_to_all | solution.py:350
  27.7 3.5 %copy-start.1 = (f32[128,8,128]{2,1,0:T(8,128)}, f32[128,8,128]{2,1,0:T(8,128)S(1)}, u32[]{:S(2)}) copy-start(f32[128,8,128]{2,1,0:T(8,128)S(1)} %all-to-all-done) | copy-start | bytes 1572868
  31.1 7.6 %copy-start.3 = (s32[1024,96]{0,1:T(8,128)S(1)}, s32[1024,96]{0,1:T(8,128)}, u32[]{:S(2)}) copy-start(s32[1024,96]{0,1:T(8,128)} %param.8) | copy-start | bytes 1179652
  31.2 7.6 %copy-start.4 = (s32[1,128]{1,0:T(1,128)S(1)}, s32[1,128]{1,0:T(1,128)}, u32[]{:S(2)}) copy-start(s32[1,128]{1,0:T(1,128)} %fills_ref.1) | copy-start | bytes 1540
  31.2 45.3 %all-to-all-start.1 = ((f32[128,8,768]{2,1,0:T(8,128)}), f32[128,8,768]{2,1,0:T(8,128)S(1)}, u32[]{:S(2)}, u32[]{:S(2)}) async-start(f32[128,8,768]{2,1,0:T(8,128)} %bitcast.38), calls=%async_computation.1 | async-start | bytes 6291456 | tf_op jit(solution)/shard_map/all_to_all | solution.py:367
  35.6 3.2 %collective-permute-start = (f32[128,8,128]{2,1,0:T(8,128)}, f32[128,8,128]{2,1,0:T(8,128)}, u32[]{:S(2)}, u32[]{:S(2)}) collective-permute-start(f32[128,8,128]{2,1,0:T(8,128)} %copy-done.1), channel_id=1, source_target_pairs={{0,16},{16,0},{32,48},{48,32},{64,80},{80,64},{96,112},{112,96},{1... | collective-permute-start | bytes 1572872 | tf_op jit(solution)/shard_map/ppermute | solution.py:351
  38.8 1.9 %copy-start = (f32[1024,768]{1,0:T(8,128)S(1)}, f32[1024,768]{1,0:T(8,128)}, u32[]{:S(2)}) copy-start(f32[1024,768]{1,0:T(8,128)} %param.6) | copy-start | bytes 9437188
  40.7 1.0 %copy-start.2 = (f32[128,8,128]{2,1,0:T(8,128)S(1)}, f32[128,8,128]{2,1,0:T(8,128)}, u32[]{:S(2)}) copy-start(f32[128,8,128]{2,1,0:T(8,128)} %copy-done.1) | copy-start | bytes 1572868

commit v7 on v6

--- a/solution.py
+++ b/solution.py
@@ -194,8 +194,6 @@
             pltpu.make_async_copy(a_hbm.at[pairs], a_ref.at[pairs], sems.at[k, 0]),
             pltpu.make_async_copy(vt_hbm.at[feats, sure], vt_ref.at[feats, sure], sems.at[k, 1]),
         ]
-        if k == 0:
-            copies.append(pltpu.make_async_copy(list_hbm, list_ref, sems.at[k, 2]))
         if hi == tiles:
             copies.append(pltpu.make_async_copy(w_hbm, w_ref, sems.at[k, 2]))
         for copy in copies:
@@ -235,8 +233,12 @@
         acc_ref[0:8, cut] += jnp.sum((resid * resid).reshape(16, 8, wide), axis=0)
         acc_ref[8:9, cut] += least
 
+    order = pltpu.make_async_copy(list_hbm, list_ref, sems.at[0, 2])
+    order.start()
     waiting = fetch(0)
     acc_ref[...] = jnp.zeros_like(acc_ref)
+    order.wait()
+    gather(0)
     for k, (lo, hi) in enumerate(STAGES):
         for copy in waiting:
             copy.wait()
@@ -244,8 +246,6 @@
             waiting = fetch(k + 1)
         for block in range(lo, hi):
             for t in range(3):
-                if block == 0 and t == 2:
-                    gather(0)
                 score(block, t)
             if hi == tiles:
                 share = rows // 8 // (hi - lo) + 1
@@ -257,6 +257,12 @@
                         total += err * err
                     part_ref[d * 8 : (d + 1) * 8, :] = total
 
+    live = live_ref[...] != 0
+    coded = [
+        jnp.sum(part_ref[h * LANES : (h + 1) * LANES, :].T, axis=0, keepdims=True) for h in range(rows // LANES)
+    ]
+    coded_ref[...] = jnp.where(live, jnp.concatenate(coded, axis=0), 0.0)
+
     @pl.when(list_ref[list_ref.shape[0] - 1] > wide)
     def _():
         rest = slice(sure.stop, rows)
@@ -269,17 +275,12 @@
 
     best = jnp.sum(acc_ref[0:8, :], axis=0, keepdims=True) + acc_ref[8:9, :]
     pos = pos_ref[...]
-    live = live_ref[...] != 0
     found = jnp.zeros(pos.shape, jnp.float32)
     for h in range(rows // LANES):
         source = jnp.broadcast_to(best[:, h * LANES : (h + 1) * LANES], pos.shape)
         lane = jnp.take_along_axis(source, pos & (LANES - 1), axis=1, mode="promise_in_bounds")
         found = jnp.where(pos // LANES == h, lane, found)
-    coded = [
-        jnp.sum(part_ref[h * LANES : (h + 1) * LANES, :].T, axis=0, keepdims=True) for h in range(rows // LANES)
-    ]
-    coded_ref[...] = jnp.where(live, jnp.concatenate(coded, axis=0), 0.0)
-    best_ref[...] = jnp.where(live, found, 0.0)
+    best_ref[...] = jnp.where(live_ref[...] != 0, found, 0.0)
 
 
 def pack_kernel(ids_hbm, book_hbm, lists_hbm, out_hbm, lists_ref, ids_ref, book_ref, out_ref, sems):

time: 90.2 us -> 89.6 us (level)
  no operation moved by 1% of the time
where the time goes in v7:
time: 89.6 us; the launch traced here: 89.2 us
  Pallas kernels  34.6 us (39%)
  waiting for transfers between devices  33.1 us (37%)
  starting transfers between devices  17.2 us (19%)
  local copies, waits for them, and re-layouts  3.1 us (3%)
    all_to_all x1, waiting for transfers between devices, local(): lax.all_to_all(picked.reshape(devices, cap, width), BOTH, 0, 0, tiled=True)  17.4 us
    pallas_call x1, Pallas kernels, local(): pl.pallas_call(prep_kernel, in_specs=[smem, smem, vmem, vmem, vmem, vmem,...  17.3 us
    all_to_all x1, waiting for transfers between devices, local(): got = lax.all_to_all(sent, BOTH, 0, 0, tiled=True)  13.8 us
    pallas_call x1, Pallas kernels, local(): pl.pallas_call(score_kernel, in_specs=[hbm, hbm, hbm, vmem, hbm, vmem, vm...  12.6 us
    all_to_all x1, starting transfers between devices, local(): got = lax.all_to_all(sent, BOTH, 0, 0, tiled=True)  11.5 us
    all_to_all x1, starting transfers between devices, local(): lax.all_to_all(picked.reshape(devices, cap, width), BOTH, 0, 0, tiled=True)  4.41 us
    pallas_call x1, Pallas kernels, local(): pl.pallas_call(pick_kernel, in_specs=[smem, vmem], out_specs=hbm, out_sha...  3.03 us
    unnamed x10, local copies, waits for them, and re-layouts  2.95 us
  transfers between devices with their start and end apart: 3, of which 3 were waited for; matrix products, arithmetic and copies ran while one was open for 0% of the time, Pallas kernels for 19%

profile of v7, /device:TPU:1, one launch (start us, length us, event | category | flops | bytes accessed | tf_op | source)
XLA Modules:
  0.0 89.2 jit_solution(7521547658903343673)
XLA Ops:
  0.6 1.7 %pack.1 = (f32[128,8,128]{2,1,0:T(8,128)}, f32[3072,128]{1,0:T(8,128)S(1)}) custom-call(s32[8,128]{1,0:T(8,128)} %bitcast.41, f32[96,128]{1,0:T(8,128)} %bitcast.40, f32[3072,128]{1,0:T(8,128)} %bitcast.39), custom_call_target="tpu_custom_call" | custom-call | tf_op jit(solution)/shard_map/pack/pallas_call | solution.py:330
  2.3 11.5 %all-to-all-start = ((f32[128,8,128]{2,1,0:T(8,128)}), f32[128,8,128]{2,1,0:T(8,128)S(1)}, u32[]{:S(2)}, u32[]{:S(2)}) async-start(f32[128,8,128]{2,1,0:T(8,128)} %get-tuple-element.12), calls=%async_computation | async-start | bytes 1048576 | tf_op jit(solution)/shard_map/all_to_all | solution.py:351
  13.8 13.8 %all-to-all-done = f32[128,8,128]{2,1,0:T(8,128)S(1)} async-done(((f32[128,8,128]{2,1,0:T(8,128)}), f32[128,8,128]{2,1,0:T(8,128)S(1)}, u32[]{:S(2)}, u32[]{:S(2)}) %all-to-all-start) | async-done | bytes 524320 | tf_op jit(solution)/shard_map/all_to_all | solution.py:351
  27.7 0.0 copy-start.1
  27.7 0.1 slice.4
  27.7 0.3 convert_reduce_fusion
  28.0 0.1 convert_element_type.8
  28.1 3.0 %pick.1 = f32[6144,128]{1,0:T(8,128)} custom-call(s32[1024]{0:T(1024)S(1)} %fusion.2.start_ref, f32[3072,128]{1,0:T(8,128)S(1)} %get-tuple-element.16.cent_ref), custom_call_target="tpu_custom_call" | custom-call | tf_op jit(solution)/shard_map/pick/pallas_call | solution.py:358
  31.1 0.0 copy-start.3
  31.2 0.0 copy-start.4
  31.2 0.0 copy-done.1
  31.2 4.4 %all-to-all-start.1 = ((f32[128,8,768]{2,1,0:T(8,128)}), f32[128,8,768]{2,1,0:T(8,128)S(1)}, u32[]{:S(2)}, u32[]{:S(2)}) async-start(f32[128,8,768]{2,1,0:T(8,128)} %bitcast.38), calls=%async_computation.1 | async-start | bytes 6291456 | tf_op jit(solution)/shard_map/all_to_all | solution.py:368
  35.6 1.3 %collective-permute-start = (f32[128,8,128]{2,1,0:T(8,128)}, f32[128,8,128]{2,1,0:T(8,128)}, u32[]{:S(2)}, u32[]{:S(2)}) collective-permute-start(f32[128,8,128]{2,1,0:T(8,128)} %copy-done.1), channel_id=1, source_target_pairs={{0,16},{16,0},{32,48},{48,32},{64,80},{80,64},{96,112},{112,96},{1... | collective-permute-start | bytes 1572872 | tf_op jit(solution)/shard_map/ppermute | solution.py:352
  36.9 1.9 %collective-permute-done = f32[128,8,128]{2,1,0:T(8,128)} collective-permute-done((f32[128,8,128]{2,1,0:T(8,128)}, f32[128,8,128]{2,1,0:T(8,128)}, u32[]{:S(2)}, u32[]{:S(2)}) %collective-permute-start) | collective-permute-done | bytes 524320 | tf_op jit(solution)/shard_map/ppermute | solution.py:352
  38.8 0.0 copy-done.3
  38.8 0.0 copy-done.4
  38.8 0.0 copy-start
  38.8 1.9 %copy-done = f32[1024,768]{1,0:T(8,128)S(1)} copy-done((f32[1024,768]{1,0:T(8,128)S(1)}, f32[1024,768]{1,0:T(8,128)}, u32[]{:S(2)}) %copy-start) | copy-done | bytes 3145752
  40.7 0.0 copy-start.2
  40.7 1.0 %copy-done.2 = f32[128,8,128]{2,1,0:T(8,128)S(1)} copy-done((f32[128,8,128]{2,1,0:T(8,128)S(1)}, f32[128,8,128]{2,1,0:T(8,128)}, u32[]{:S(2)}) %copy-start.2) | copy-done | bytes 524312
  41.7 17.3 %prep.1 = (f32[768,1024]{1,0:T(8,128)}, f32[6144,128]{1,0:T(8,128)}, bf16[48,256,128]{2,1,0:T(8,128)(2,1)}, s32[1024]{0:T(1024)}, s32[8,128]{1,0:T(8,128)S(1)}, /*index=5*/s32[8,128]{1,0:T(8,128)S(1)}) custom-call(s32[1]{0:T(128)} %bitcast.core_ref, s32[128]{0:T(128)S(1)} %bitcast.37, s32[1,128]{1,0:T(1,128)S(1)} %copy-done.4, f32[6144,128]{1,0:T(8,128)S(1)} %bitcast.34, ...), custom_call_target="tpu_custom_call" | custom-call | tf_op jit(solution)/shard_map/prep/pallas_call | solution.py:373
  59.0 17.4 %all-to-all-done.1 = f32[128,8,768]{2,1,0:T(8,128)S(1)} async-done(((f32[128,8,768]{2,1,0:T(8,128)}), f32[128,8,768]{2,1,0:T(8,128)S(1)}, u32[]{:S(2)}, u32[]{:S(2)}) %all-to-all-start.1) | async-done | bytes 3145760 | tf_op jit(solution)/shard_map/all_to_all | solution.py:368
  76.4 12.6 %score.1 = (f32[8,128]{1,0:T(8,128)}, f32[8,128]{1,0:T(8,128)}) custom-call(s32[1024]{0:T(1024)} %get-tuple-element.13.list_hbm, f32[768,1024]{1,0:T(8,128)} %get-tuple-element.14.vt_hbm, f32[6144,128]{1,0:T(8,128)} %get-tuple-element.15.w_hbm, f32[6144,128]{1,0:T(8,128)S(1)} %bitcast.33, bf16[48,256,128]{2,1,0:T(8,128)(2,1)} %get-tuple-element.17.a_hbm, ...), custom_call_target="tpu_custom_call" | custom-call | tf_op jit(solution)/shard_map/score/pallas_call | solution.py:405
  (1 shorter events, 0.0 us)
Async XLA Ops:
  2.3 25.4 %all-to-all-start = ((f32[128,8,128]{2,1,0:T(8,128)}), f32[128,8,128]{2,1,0:T(8,128)S(1)}, u32[]{:S(2)}, u32[]{:S(2)}) async-start(f32[128,8,128]{2,1,0:T(8,128)} %get-tuple-element.12), calls=%async_computation | async-start | bytes 1048576 | tf_op jit(solution)/shard_map/all_to_all | solution.py:351
  27.7 3.5 %copy-start.1 = (f32[128,8,128]{2,1,0:T(8,128)}, f32[128,8,128]{2,1,0:T(8,128)S(1)}, u32[]{:S(2)}) copy-start(f32[128,8,128]{2,1,0:T(8,128)S(1)} %all-to-all-done) | copy-start | bytes 1572868
  31.1 7.6 %copy-start.3 = (s32[1024,96]{0,1:T(8,128)S(1)}, s32[1024,96]{0,1:T(8,128)}, u32[]{:S(2)}) copy-start(s32[1024,96]{0,1:T(8,128)} %param.8) | copy-start | bytes 1179652
  31.2 7.6 %copy-start.4 = (s32[1,128]{1,0:T(1,128)S(1)}, s32[1,128]{1,0:T(1,128)}, u32[]{:S(2)}) copy-start(s32[1,128]{1,0:T(1,128)} %fills_ref.1) | copy-start | bytes 1540
  31.2 45.3 %all-to-all-start.1 = ((f32[128,8,768]{2,1,0:T(8,128)}), f32[128,8,768]{2,1,0:T(8,128)S(1)}, u32[]{:S(2)}, u32[]{:S(2)}) async-start(f32[128,8,768]{2,1,0:T(8,128)} %bitcast.38), calls=%async_computation.1 | async-start | bytes 6291456 | tf_op jit(solution)/shard_map/all_to_all | solution.py:368
  35.6 3.2 %collective-permute-start = (f32[128,8,128]{2,1,0:T(8,128)}, f32[128,8,128]{2,1,0:T(8,128)}, u32[]{:S(2)}, u32[]{:S(2)}) collective-permute-start(f32[128,8,128]{2,1,0:T(8,128)} %copy-done.1), channel_id=1, source_target_pairs={{0,16},{16,0},{32,48},{48,32},{64,80},{80,64},{96,112},{112,96},{1... | collective-permute-start | bytes 1572872 | tf_op jit(solution)/shard_map/ppermute | solution.py:352
  38.8 1.9 %copy-start = (f32[1024,768]{1,0:T(8,128)S(1)}, f32[1024,768]{1,0:T(8,128)}, u32[]{:S(2)}) copy-start(f32[1024,768]{1,0:T(8,128)} %param.6) | copy-start | bytes 9437188
  40.7 1.0 %copy-start.2 = (f32[128,8,128]{2,1,0:T(8,128)S(1)}, f32[128,8,128]{2,1,0:T(8,128)}, u32[]{:S(2)}) copy-start(f32[128,8,128]{2,1,0:T(8,128)} %copy-done.1) | copy-start | bytes 1572868

commit v8 on v7

--- a/solution.py
+++ b/solution.py
@@ -150,14 +150,9 @@
     slots = words // tiles
     copies = []
     for part in range(PARTS):
-
-        def some(i, carry, part=part):
-            for k in range(32):
-                row = cent_ref[pl.ds(start_ref[part * slots + i * 32 + k], tiles, stride=8), :]
-                out_ref[pl.ds(part * words + (i * 4 + k // 8) * (8 * tiles) + k % 8, tiles, stride=8), :] = row
-            return carry
-
-        lax.fori_loop(0, slots // 32, some, 0)
+        for k in range(slots):
+            row = cent_ref[pl.ds(start_ref[part * slots + k], tiles, stride=8), :]
+            out_ref[pl.ds(part * words + k // 8 * (8 * tiles) + k % 8, tiles, stride=8), :] = row
         cut = slice(part * words, (part + 1) * words)
         copies.append(pltpu.make_async_copy(out_ref.at[cut], out_hbm.at[cut], sems.at[part]))
         copies[-1].start()

time: 89.6 us -> 89.4 us (level)
  no operation moved by 1% of the time
where the time goes in v8:
time: 89.4 us; the launch traced here: 88.9 us
  Pallas kernels  34.3 us (38%)
  waiting for transfers between devices  33.1 us (37%)
  starting transfers between devices  17.2 us (19%)
  local copies, waits for them, and re-layouts  3.1 us (3%)
    all_to_all x1, waiting for transfers between devices, local(): lax.all_to_all(picked.reshape(devices, cap, width), BOTH, 0, 0, tiled=True)  17.4 us
    pallas_call x1, Pallas kernels, local(): pl.pallas_call(prep_kernel, in_specs=[smem, smem, vmem, vmem, vmem, vmem,...  17.3 us
    all_to_all x1, waiting for transfers between devices, local(): got = lax.all_to_all(sent, BOTH, 0, 0, tiled=True)  13.8 us
    pallas_call x1, Pallas kernels, local(): pl.pallas_call(score_kernel, in_specs=[hbm, hbm, hbm, vmem, hbm, vmem, vm...  12.6 us
    all_to_all x1, starting transfers between devices, local(): got = lax.all_to_all(sent, BOTH, 0, 0, tiled=True)  11.5 us
    all_to_all x1, starting transfers between devices, local(): lax.all_to_all(picked.reshape(devices, cap, width), BOTH, 0, 0, tiled=True)  4.41 us
    unnamed x10, local copies, waits for them, and re-layouts  2.95 us
    pallas_call x1, Pallas kernels, local(): pl.pallas_call(pick_kernel, in_specs=[smem, vmem], out_specs=hbm, out_sha...  2.77 us
  transfers between devices with their start and end apart: 3, of which 3 were waited for; matrix products, arithmetic and copies ran while one was open for 0% of the time, Pallas kernels for 19%

profile of v8, /device:TPU:1, one launch (start us, length us, event | category | flops | bytes accessed | tf_op | source)
XLA Modules:
  0.0 88.9 jit_solution(9382389979052249827)
XLA Ops:
  0.6 1.7 %pack.1 = (f32[128,8,128]{2,1,0:T(8,128)}, f32[3072,128]{1,0:T(8,128)S(1)}) custom-call(s32[8,128]{1,0:T(8,128)} %bitcast.41, f32[96,128]{1,0:T(8,128)} %bitcast.40, f32[3072,128]{1,0:T(8,128)} %bitcast.39), custom_call_target="tpu_custom_call" | custom-call | tf_op jit(solution)/shard_map/pack/pallas_call | solution.py:325
  2.3 11.5 %all-to-all-start = ((f32[128,8,128]{2,1,0:T(8,128)}), f32[128,8,128]{2,1,0:T(8,128)S(1)}, u32[]{:S(2)}, u32[]{:S(2)}) async-start(f32[128,8,128]{2,1,0:T(8,128)} %get-tuple-element.12), calls=%async_computation | async-start | bytes 1048576 | tf_op jit(solution)/shard_map/all_to_all | solution.py:346
  13.8 13.8 %all-to-all-done = f32[128,8,128]{2,1,0:T(8,128)S(1)} async-done(((f32[128,8,128]{2,1,0:T(8,128)}), f32[128,8,128]{2,1,0:T(8,128)S(1)}, u32[]{:S(2)}, u32[]{:S(2)}) %all-to-all-start) | async-done | bytes 524320 | tf_op jit(solution)/shard_map/all_to_all | solution.py:346
  27.7 0.0 copy-start.1
  27.7 0.1 slice.4
  27.7 0.3 convert_reduce_fusion
  28.0 0.1 convert_element_type.8
  28.1 2.8 %pick.1 = f32[6144,128]{1,0:T(8,128)} custom-call(s32[1024]{0:T(1024)S(1)} %fusion.2.start_ref, f32[3072,128]{1,0:T(8,128)S(1)} %get-tuple-element.16.cent_ref), custom_call_target="tpu_custom_call" | custom-call | tf_op jit(solution)/shard_map/pick/pallas_call | solution.py:353
  30.9 0.0 copy-start.3
  30.9 0.0 copy-start.4
  30.9 0.0 copy-done.1
  30.9 4.4 %all-to-all-start.1 = ((f32[128,8,768]{2,1,0:T(8,128)}), f32[128,8,768]{2,1,0:T(8,128)S(1)}, u32[]{:S(2)}, u32[]{:S(2)}) async-start(f32[128,8,768]{2,1,0:T(8,128)} %bitcast.38), calls=%async_computation.1 | async-start | bytes 6291456 | tf_op jit(solution)/shard_map/all_to_all | solution.py:363
  35.3 1.3 %collective-permute-start = (f32[128,8,128]{2,1,0:T(8,128)}, f32[128,8,128]{2,1,0:T(8,128)}, u32[]{:S(2)}, u32[]{:S(2)}) collective-permute-start(f32[128,8,128]{2,1,0:T(8,128)} %copy-done.1), channel_id=1, source_target_pairs={{0,16},{16,0},{32,48},{48,32},{64,80},{80,64},{96,112},{112,96},{1... | collective-permute-start | bytes 1572872 | tf_op jit(solution)/shard_map/ppermute | solution.py:347
  36.6 1.9 %collective-permute-done = f32[128,8,128]{2,1,0:T(8,128)} collective-permute-done((f32[128,8,128]{2,1,0:T(8,128)}, f32[128,8,128]{2,1,0:T(8,128)}, u32[]{:S(2)}, u32[]{:S(2)}) %collective-permute-start) | collective-permute-done | bytes 524320 | tf_op jit(solution)/shard_map/ppermute | solution.py:347
  38.5 0.0 copy-done.3
  38.5 0.0 copy-done.4
  38.5 0.0 copy-start
  38.5 1.9 %copy-done = f32[1024,768]{1,0:T(8,128)S(1)} copy-done((f32[1024,768]{1,0:T(8,128)S(1)}, f32[1024,768]{1,0:T(8,128)}, u32[]{:S(2)}) %copy-start) | copy-done | bytes 3145752
  40.4 0.0 copy-start.2
  40.4 1.0 %copy-done.2 = f32[128,8,128]{2,1,0:T(8,128)S(1)} copy-done((f32[128,8,128]{2,1,0:T(8,128)S(1)}, f32[128,8,128]{2,1,0:T(8,128)}, u32[]{:S(2)}) %copy-start.2) | copy-done | bytes 524312
  41.4 17.3 %prep.1 = (f32[768,1024]{1,0:T(8,128)}, f32[6144,128]{1,0:T(8,128)}, bf16[48,256,128]{2,1,0:T(8,128)(2,1)}, s32[1024]{0:T(1024)}, s32[8,128]{1,0:T(8,128)S(1)}, /*index=5*/s32[8,128]{1,0:T(8,128)S(1)}) custom-call(s32[1]{0:T(128)} %bitcast.core_ref, s32[128]{0:T(128)S(1)} %bitcast.37, s32[1,128]{1,0:T(1,128)S(1)} %copy-done.4, f32[6144,128]{1,0:T(8,128)S(1)} %bitcast.34, ...), custom_call_target="tpu_custom_call" | custom-call | tf_op jit(solution)/shard_map/prep/pallas_call | solution.py:368
  58.8 17.4 %all-to-all-done.1 = f32[128,8,768]{2,1,0:T(8,128)S(1)} async-done(((f32[128,8,768]{2,1,0:T(8,128)}), f32[128,8,768]{2,1,0:T(8,128)S(1)}, u32[]{:S(2)}, u32[]{:S(2)}) %all-to-all-start.1) | async-done | bytes 3145760 | tf_op jit(solution)/shard_map/all_to_all | solution.py:363
  76.2 12.6 %score.1 = (f32[8,128]{1,0:T(8,128)}, f32[8,128]{1,0:T(8,128)}) custom-call(s32[1024]{0:T(1024)} %get-tuple-element.13.list_hbm, f32[768,1024]{1,0:T(8,128)} %get-tuple-element.14.vt_hbm, f32[6144,128]{1,0:T(8,128)} %get-tuple-element.15.w_hbm, f32[6144,128]{1,0:T(8,128)S(1)} %bitcast.33, bf16[48,256,128]{2,1,0:T(8,128)(2,1)} %get-tuple-element.17.a_hbm, ...), custom_call_target="tpu_custom_call" | custom-call | tf_op jit(solution)/shard_map/score/pallas_call | solution.py:400
  (1 shorter events, 0.0 us)
Async XLA Ops:
  2.3 25.4 %all-to-all-start = ((f32[128,8,128]{2,1,0:T(8,128)}), f32[128,8,128]{2,1,0:T(8,128)S(1)}, u32[]{:S(2)}, u32[]{:S(2)}) async-start(f32[128,8,128]{2,1,0:T(8,128)} %get-tuple-element.12), calls=%async_computation | async-start | bytes 1048576 | tf_op jit(solution)/shard_map/all_to_all | solution.py:346
  27.7 3.3 %copy-start.1 = (f32[128,8,128]{2,1,0:T(8,128)}, f32[128,8,128]{2,1,0:T(8,128)S(1)}, u32[]{:S(2)}) copy-start(f32[128,8,128]{2,1,0:T(8,128)S(1)} %all-to-all-done) | copy-start | bytes 1572868
  30.9 7.6 %copy-start.3 = (s32[1024,96]{0,1:T(8,128)S(1)}, s32[1024,96]{0,1:T(8,128)}, u32[]{:S(2)}) copy-start(s32[1024,96]{0,1:T(8,128)} %param.8) | copy-start | bytes 1179652
  30.9 7.6 %copy-start.4 = (s32[1,128]{1,0:T(1,128)S(1)}, s32[1,128]{1,0:T(1,128)}, u32[]{:S(2)}) copy-start(s32[1,128]{1,0:T(1,128)} %fills_ref.1) | copy-start | bytes 1540
  30.9 45.3 %all-to-all-start.1 = ((f32[128,8,768]{2,1,0:T(8,128)}), f32[128,8,768]{2,1,0:T(8,128)S(1)}, u32[]{:S(2)}, u32[]{:S(2)}) async-start(f32[128,8,768]{2,1,0:T(8,128)} %bitcast.38), calls=%async_computation.1 | async-start | bytes 6291456 | tf_op jit(solution)/shard_map/all_to_all | solution.py:363
  35.3 3.2 %collective-permute-start = (f32[128,8,128]{2,1,0:T(8,128)}, f32[128,8,128]{2,1,0:T(8,128)}, u32[]{:S(2)}, u32[]{:S(2)}) collective-permute-start(f32[128,8,128]{2,1,0:T(8,128)} %copy-done.1), channel_id=1, source_target_pairs={{0,16},{16,0},{32,48},{48,32},{64,80},{80,64},{96,112},{112,96},{1... | collective-permute-start | bytes 1572872 | tf_op jit(solution)/shard_map/ppermute | solution.py:347
  38.5 1.9 %copy-start = (f32[1024,768]{1,0:T(8,128)S(1)}, f32[1024,768]{1,0:T(8,128)}, u32[]{:S(2)}) copy-start(f32[1024,768]{1,0:T(8,128)} %param.6) | copy-start | bytes 9437188
  40.4 1.0 %copy-start.2 = (f32[128,8,128]{2,1,0:T(8,128)S(1)}, f32[128,8,128]{2,1,0:T(8,128)}, u32[]{:S(2)}) copy-start(f32[128,8,128]{2,1,0:T(8,128)} %copy-done.1) | copy-start | bytes 1572868
